TPU v7x, 32 devices: a whole 2x2x4 slice. The times are simulated.
32 devices in a mesh: rep: 4 (over x, core), mx: 2 (over y), my: 4 (over z).
Axes of the slice: x: 2, y: 2, z: 4, core: 2. Of those that a mesh axis runs over, the one named last changes fastest.
Arguments:
- coefficients: bfloat16 [2, 384, 384, 384], P(None, 'mx', 'my'), may hold values from -7.5 to 7.5
- noise_field: bfloat16 [128, 2, 1536, 1536], P(('rep', 'mx'), None, 'my'), may hold values from -96 to 96
- mode_table: bfloat16 [384, 1536], replicated, may hold values from -0.3125 to 0.3125
Outputs:
- update: bfloat16 [2, 384, 384, 384], P(None, 'mx', 'my', 'rep')
All inputs are finite; a program needn't handle non-finite values.
Results may differ from a plain program's by a relative error of at most 0.008.
Values may be sent and summed in bfloat16 or wider, within the bound.
A program may use at most 384 MiB of HBM per device.

v0:
```python
import jax
import jax.numpy as jnp
from jax import lax
from jax.experimental import pallas as pl
from jax.experimental.pallas import tpu as pltpu
from jax.sharding import PartitionSpec as P

DAMPING = 0.25
MESH = pl.DeviceIdType.MESH
NT = (((1,), (1,)), ((), ()))


def plain_body(coefficients, noise_field, mode_table):
    rep_index = lax.axis_index("rep")
    col_index = lax.axis_index("my")
    rep_count = lax.axis_size("rep")
    row_count = lax.axis_size("mx")
    col_count = lax.axis_size("my")
    planes_dev = noise_field.shape[0]
    planes_rep = planes_dev * row_count
    planes_all = planes_rep * rep_count
    mode_count = mode_table.shape[0]
    point_count = mode_table.shape[1]
    slab_first = point_count // 2 - planes_all // 2
    row_block = mode_count // row_count
    col_block = mode_count // col_count
    point_block = point_count // col_count
    own_block = mode_count // rep_count
    slab_own = lax.dynamic_slice_in_dim(
        mode_table, slab_first + rep_index * planes_rep, planes_rep, 1
    )
    zmodes = jnp.einsum(
        "pabk,kz->zpba", coefficients, slab_own, preferred_element_type=jnp.float32
    ).astype(jnp.bfloat16)
    zmodes = zmodes.reshape(planes_rep, 2, col_block * row_block)
    spread = lax.all_to_all(zmodes, "mx", split_axis=0, concat_axis=2, tiled=True)
    grouped = spread.reshape(planes_dev, 2, row_count, col_block, row_block)
    tiled_table = mode_table.reshape(row_count, row_block, point_count)
    own_points = lax.dynamic_slice_in_dim(tiled_table, col_index * point_block, point_block, 2)
    block_part = jnp.einsum(
        "zpsal,slx->zpax",
        lax.all_gather(grouped, "my", axis=3, tiled=True),
        own_points,
        preferred_element_type=jnp.float32,
    ).astype(jnp.bfloat16)
    wave_field = jnp.einsum(
        "zpax,ay->zpxy", block_part, mode_table, preferred_element_type=jnp.float32
    )
    wave_real = wave_field[:, 0]
    wave_imag = wave_field[:, 1]
    density = wave_real * wave_real + wave_imag * wave_imag
    noise_wide = noise_field.astype(jnp.float32)
    drive_term = jnp.stack(
        [
            density * (wave_imag - DAMPING * wave_real) + noise_wide[:, 0],
            density * (-wave_real - DAMPING * wave_imag) + noise_wide[:, 1],
        ],
        1,
    ).astype(jnp.bfloat16)
    proj_columns = jnp.einsum(
        "zpxy,ny->zpnx", drive_term, mode_table, preferred_element_type=jnp.float32
    ).astype(jnp.bfloat16)
    block_part = lax.all_to_all(proj_columns, "my", split_axis=2, concat_axis=3, tiled=True)
    folded = jnp.einsum(
        "zpax,slx->zpsal", block_part, tiled_table, preferred_element_type=jnp.float32
    ).astype(jnp.bfloat16)
    proj_rows = folded.reshape(
        block_part.shape[0], block_part.shape[1], row_count * col_block * row_block
    )
    gathered_rows = lax.all_to_all(proj_rows, "mx", split_axis=2, concat_axis=0, tiled=True)
    slab_back = lax.dynamic_slice_in_dim(mode_table, rep_index * own_block, own_block, 0)[
        :, slab_first : slab_first + planes_all
    ]
    portion = lax.all_gather(gathered_rows, "rep", axis=0, tiled=True)
    plane_grid = portion.reshape(portion.shape[0], 2, col_block, row_block)
    summed = jnp.einsum("zpba,nz->pabn", plane_grid, slab_back, preferred_element_type=jnp.float32)
    return summed.astype(jnp.bfloat16)

def slab_kernel(own_ref, noise_ref, table_ref, turned_ref, out_ref, modes, parts, landed, noise,
                halves, own_sem, noise_sem, gather_recv, gather_send, sum_recv, sum_send,
                half_recv, half_send, last_recv, last_send):
    count = lax.axis_size("my")
    me = lax.axis_index("my")
    row_count = lax.axis_size("mx")
    row = lax.axis_index("mx")
    rep_count = lax.axis_size("rep")
    rep = lax.axis_index("rep")
    planes = own_ref.shape[0] // row_count
    block = own_ref.shape[2]
    row_block = own_ref.shape[3]
    offsets = [(dr, dh) for dr in range(rep_count) for dh in range(row_count)]
    mode_count, point_count = table_ref.shape
    chunk = max(c for c in (512, 256, 128) if point_count % c == 0)
    up = {"my": me + 1}
    down = {"my": me - 1}
    has_up = me < count - 1
    has_down = me > 0

    barrier = pltpu.get_barrier_semaphore()

    @pl.when(has_up)
    def _():
        pl.semaphore_signal(barrier, inc=1, device_id=up, device_id_type=MESH)

    @pl.when(has_down)
    def _():
        pl.semaphore_signal(barrier, inc=1, device_id=down, device_id_type=MESH)

    for dr, dh in offsets[1:]:
        pl.semaphore_signal(
            barrier, inc=1,
            device_id={"rep": lax.rem(rep + dr, rep_count), "mx": lax.rem(row + dh, row_count)},
            device_id_type=MESH,
        )

    def rows(j):
        return pl.ds(pl.multiple_of(j * block, block), block)

    def own_copy():
        return pltpu.make_async_copy(
            own_ref.at[pl.ds(row * planes, planes)], halves.at[:, row], own_sem
        )

    def half_copy(p, dh, source):
        target = lax.rem(row + dh, row_count)
        return pltpu.make_async_remote_copy(
            src_ref=own_ref.at[target * planes + p],
            dst_ref=halves.at[p, source],
            send_sem=half_send.at[p, dh],
            recv_sem=half_recv.at[p, dh],
            device_id={"mx": target},
            device_id_type=MESH,
        )

    def last_copy(p, at, received):
        dr, dh = offsets[at]
        target = lax.rem(row + dh, row_count)
        if received:
            from_rep = lax.rem(rep + rep_count - dr, rep_count)
            from_row = lax.rem(row + row_count - dh, row_count)
        else:
            from_rep, from_row = rep, row
        plane = (from_rep * row_count + from_row) * planes + p
        if at == 0:
            return pltpu.make_async_copy(halves.at[p, row], out_ref.at[plane], last_send.at[p, 0])
        return pltpu.make_async_remote_copy(
            src_ref=halves.at[p, target],
            dst_ref=out_ref.at[plane],
            send_sem=last_send.at[p, at],
            recv_sem=last_recv.at[p, at],
            device_id={"rep": lax.rem(rep + dr, rep_count), "mx": target},
            device_id_type=MESH,
        )

    def noise_copy(p):
        slot = lax.rem(p, 2)
        return pltpu.make_async_copy(noise_ref.at[p], noise.at[slot], noise_sem.at[slot])

    def gather_copy(p, j, way):
        return pltpu.make_async_remote_copy(
            src_ref=modes.at[p, :, rows(j)],
            dst_ref=modes.at[p, :, rows(j)],
            send_sem=gather_send.at[p, way, j],
            recv_sem=gather_recv.at[p, j],
            device_id=down if way else up,
            device_id_type=MESH,
        )

    def sum_copy(p, j, way, slot):
        return pltpu.make_async_remote_copy(
            src_ref=parts.at[p, :, rows(j)],
            dst_ref=landed.at[p, slot],
            send_sem=sum_send.at[p, way, j],
            recv_sem=sum_recv.at[p, slot],
            device_id=down if way else up,
            device_id_type=MESH,
        )

    own_copy().start()
    noise_copy(0).start()
    if planes > 1:
        noise_copy(1).start()

    pl.semaphore_wait(barrier, has_up.astype(jnp.int32) + has_down.astype(jnp.int32) + len(offsets) - 1)

    def send_half(p, carry):
        for dh in range(1, row_count):
            half_copy(p, dh, row).start()
        return carry

    lax.fori_loop(0, planes, send_half, 0)
    own_copy().wait()

    def inside(p):
        return jnp.logical_and(p >= 0, p < planes)

    def step(s, carry):
        @pl.when(s < planes)
        def _():
            for dh in range(1, row_count):
                half_copy(s, dh, lax.rem(row + row_count - dh, row_count)).wait_recv()
            for part in range(2):
                modes[s, part, rows(me)] = jnp.concatenate(
                    [halves[s, h, part] for h in range(row_count)], 1
                )

            @pl.when(has_up)
            def _():
                gather_copy(s, me, 0).start()

            @pl.when(has_down)
            def _():
                gather_copy(s, me, 1).start()

        for far in range(1, count):
            p = s - far

            @pl.when(jnp.logical_and(inside(p), me - far >= 0))
            def _():
                gather_copy(p, me - far, 0).wait_recv()

                @pl.when(has_up)
                def _():
                    gather_copy(p, me - far, 0).start()

            @pl.when(jnp.logical_and(inside(p), me + far <= count - 1))
            def _():
                gather_copy(p, me + far, 1).wait_recv()

                @pl.when(has_down)
                def _():
                    gather_copy(p, me + far, 1).start()

        c = s - (count - 1)

        @pl.when(inside(c))
        def _():
            noise_copy(c).wait()
            slot = lax.rem(c, 2)
            turned = turned_ref[...]
            lines = [
                lax.dot_general(turned, modes[c, part], NT, preferred_element_type=jnp.float32)
                .astype(jnp.bfloat16)
                for part in range(2)
            ]
            columns = [None, None]
            for first in range(0, point_count, chunk):
                span = slice(first, first + chunk)
                table = table_ref[:, span]
                wave_real, wave_imag = [
                    jnp.dot(line, table, preferred_element_type=jnp.float32) for line in lines
                ]
                density = wave_real * wave_real + wave_imag * wave_imag
                noise_real = noise[slot, 0, :, span].astype(jnp.float32)
                noise_imag = noise[slot, 1, :, span].astype(jnp.float32)
                drive = [
                    density * (wave_imag - DAMPING * wave_real) + noise_real,
                    density * (-wave_real - DAMPING * wave_imag) + noise_imag,
                ]
                for part in range(2):
                    more = lax.dot_general(
                        table, drive[part].astype(jnp.bfloat16), NT,
                        preferred_element_type=jnp.float32,
                    )
                    columns[part] = more if first == 0 else columns[part] + more
            for part in range(2):
                parts[c, part] = jnp.dot(
                    columns[part].astype(jnp.bfloat16), turned, preferred_element_type=jnp.float32
                ).astype(jnp.bfloat16)

            @pl.when(c + 2 < planes)
            def _():
                noise_copy(c + 2).start()

        def add(p, j, slot):
            wide = parts[p, :, rows(j)].astype(jnp.float32) + landed[p, slot].astype(jnp.float32)
            parts[p, :, rows(j)] = wide.astype(jnp.bfloat16)

        rising = c - me
        for far in range(count - 1, 0, -1):
            @pl.when(jnp.logical_and(inside(rising), me + far <= count - 1))
            def _():
                j = me + far

                @pl.when(has_down)
                def _():
                    sum_copy(rising, j, 0, j).wait_recv()
                    add(rising, j, j)

                sum_copy(rising, j, 0, j).start()

        sinking = c - (count - 1 - me)
        for far in range(count - 1, 0, -1):
            @pl.when(jnp.logical_and(inside(sinking), me - far >= 0))
            def _():
                j = me - far

                @pl.when(has_up)
                def _():
                    sum_copy(sinking, j, 1, j).wait_recv()
                    add(sinking, j, j)

                sum_copy(sinking, j, 1, count if far == 1 else j).start()

        done = c - (count - 1)

        @pl.when(inside(done))
        def _():
            @pl.when(has_down)
            def _():
                sum_copy(done, me, 0, me).wait_recv()
                add(done, me, me)

            @pl.when(has_up)
            def _():
                sum_copy(done, me, 1, count).wait_recv()
                add(done, me, count)

            for part in range(2):
                whole = parts[done, part, rows(me)]
                for h in range(row_count):
                    halves[done, h, part] = whole[:, h * row_block : (h + 1) * row_block]
            for at in range(len(offsets)):
                last_copy(done, at, False).start()

        return carry

    lax.fori_loop(0, planes + 2 * count - 2, step, 0)

    def finish(p, carry):
        for j in range(count):
            @pl.when(jnp.logical_and(has_up, j <= me))
            def _():
                gather_copy(p, j, 0).wait_send()

            @pl.when(jnp.logical_and(has_down, j >= me))
            def _():
                gather_copy(p, j, 1).wait_send()

            @pl.when(j > me)
            def _():
                sum_copy(p, j, 0, j).wait_send()

            @pl.when(j < me)
            def _():
                sum_copy(p, j, 1, j).wait_send()

        for dh in range(1, row_count):
            half_copy(p, dh, row).wait_send()
        last_copy(p, 0, False).wait()
        for at in range(1, len(offsets)):
            last_copy(p, at, False).wait_send()
            last_copy(p, at, True).wait_recv()
        return carry

    lax.fori_loop(0, planes, finish, 0)


def slab_planes(own_modes, noise_field, mode_table, turned):
    count = lax.axis_size("my")
    mode_count = mode_table.shape[0]
    row_count = lax.axis_size("mx")
    rep_count = lax.axis_size("rep")
    planes_rep, _, block, row_block = own_modes.shape
    planes = planes_rep // row_count
    point_block, point_count = noise_field.shape[2:]
    vmem = pl.BlockSpec(memory_space=pltpu.VMEM)
    hbm = pl.BlockSpec(memory_space=pl.ANY)
    dma = pltpu.SemaphoreType.DMA
    flops = 8 * planes * mode_count * point_block * (point_count + mode_count)
    return pl.pallas_call(
        slab_kernel,
        out_shape=jax.ShapeDtypeStruct((planes_rep * rep_count, 2, block, row_block), jnp.bfloat16),
        in_specs=[hbm, hbm, vmem, vmem],
        out_specs=hbm,
        scratch_shapes=[
            pltpu.VMEM((planes, 2, mode_count, mode_count), jnp.bfloat16),
            pltpu.VMEM((planes, 2, mode_count, mode_count), jnp.bfloat16),
            pltpu.VMEM((planes, count + 1, 2, block, mode_count), jnp.bfloat16),
            pltpu.VMEM((2, 2, point_block, point_count), jnp.bfloat16),
            pltpu.VMEM((planes, row_count, 2, block, row_block), jnp.bfloat16),
            dma,
            dma((2,)),
            dma((planes, count)),
            dma((planes, 2, count)),
            dma((planes, count + 1)),
            dma((planes, 2, count)),
            dma((planes, row_count)),
            dma((planes, row_count)),
            dma((planes, row_count * rep_count)),
            dma((planes, row_count * rep_count)),
        ],
        compiler_params=pltpu.CompilerParams(
            collective_id=0, has_side_effects=True, vmem_limit_bytes=60 * 1024 * 1024
        ),
        cost_estimate=pl.CostEstimate(
            flops=flops, bytes_accessed=noise_field.size * 2, transcendentals=0
        ),
    )(own_modes, noise_field, mode_table, turned)


def body(coefficients, noise_field, mode_table):
    rep_index = lax.axis_index("rep")
    col_index = lax.axis_index("my")
    rep_count = lax.axis_size("rep")
    row_count = lax.axis_size("mx")
    col_count = lax.axis_size("my")
    planes_dev = noise_field.shape[0]
    planes_rep = planes_dev * row_count
    planes_all = planes_rep * rep_count
    mode_count = mode_table.shape[0]
    point_count = mode_table.shape[1]
    slab_first = point_count // 2 - planes_all // 2
    row_block = mode_count // row_count
    col_block = mode_count // col_count
    point_block = point_count // col_count
    own_block = mode_count // rep_count
    if col_block % 16 or point_block % 128 or mode_count % 128 or col_count < 2:
        return plain_body(coefficients, noise_field, mode_table)
    slab_own = lax.dynamic_slice_in_dim(
        mode_table, slab_first + rep_index * planes_rep, planes_rep, 1
    )
    zmodes = jnp.einsum(
        "pabk,kz->zpba", coefficients, slab_own, preferred_element_type=jnp.float32
    ).astype(jnp.bfloat16)
    turned = lax.dynamic_slice_in_dim(mode_table, col_index * point_block, point_block, 1).T
    plane_grid = slab_planes(zmodes, noise_field, mode_table, turned)
    slab_back = lax.dynamic_slice_in_dim(mode_table, rep_index * own_block, own_block, 0)[
        :, slab_first : slab_first + planes_all
    ]
    summed = jnp.einsum("zpba,nz->pabn", plane_grid, slab_back, preferred_element_type=jnp.float32)
    return summed.astype(jnp.bfloat16)


def solution(mesh):
    in_specs = (P(None, "mx", "my", None), P(("rep", "mx"), None, "my", None), P())
    out_specs = P(None, "mx", "my", "rep")
    return jax.shard_map(body, mesh=mesh, in_specs=in_specs, out_specs=out_specs, check_vma=False)
```

profile of v0, /device:TPU:0, one launch (start us, length us, event | category | flops | bytes accessed | tf_op | source)
XLA Modules:
  0.0 302.0 jit_solution(17672028078717098582)
XLA Ops:
  0.0 1.0 constant_dynamic-slice_fusion
  1.0 0.9 copy.10
  1.9 17.5 %fusion.4 = bf16[32,2,192,96]{3,0,2,1:T(8,128)(2,1)S(1)} fusion(bf16[2,192,96,384]{3,2,1,0:T(8,128)(2,1)} %param.3, bf16[384,1536]{1,0:T(8,128)(2,1)} %table_ref.1, s32[]{:T(128)S(6)} %select_n.10), kind=kOutput, calls=%fused_computation.4 | convolution fusion | flops 905969664 | bytes 30769156 | tf_op jit(solution)/shard_map/pabk,kz->zpba/dot_general | solution.py:423
  19.4 3.8 %copy.8 = bf16[32,2,192,96]{2,3,1,0:T(8,128)(2,1)} copy(bf16[32,2,192,96]{3,0,2,1:T(8,128)(2,1)S(1)} %fusion.4) | data formatting | bytes 4718592 | tf_op jit(solution)/shard_map/pabk,kz->zpba/dot_general | solution.py:423
  23.2 248.2 %shard_map.37 = bf16[128,2,96,192]{3,2,1,0:T(8,128)(2,1)} custom-call(bf16[32,2,96,192]{3,2,1,0:T(8,128)(2,1)} %bitcast.17, bf16[16,2,384,1536]{3,2,1,0:T(8,128)(2,1)} %noise_ref.1, bf16[384,1536]{1,0:T(8,128)(2,1)} %table_ref.1, bf16[384,384]{1,0:T(8,128)(2,1)} %bitcast.18), custom_call_target="tpu_custom_call" | custom-call | flops 36238786560 | bytes 37748736 | tf_op jit(solution)/shard_map/pallas_call | solution.py:371
  271.4 16.8 %convert_bitcast_fusion = bf16[2,192,96,96]{1,3,2,0:T(8,128)(2,1)} fusion(bf16[128,2,96,192]{3,2,1,0:T(8,128)(2,1)} %shard_map.37, bf16[384,1536]{1,0:T(8,128)(2,1)} %table_ref.1, s32[]{:T(128)S(6)} %select_n.9, s32[]{:T(128)S(6)} %add.14), kind=kOutput, calls=%fused_computation.2 | convolution fusion | flops 909508608 | bytes 19685384 | tf_op jit(solution)/shard_map/zpba,nz->pabn/dot_general | solution.py:431
  288.2 13.9 %copy.6 = bf16[2,192,96,96]{3,2,1,0:T(8,128)(2,1)} copy(bf16[2,192,96,96]{1,3,2,0:T(8,128)(2,1)} %convert_bitcast_fusion) | data formatting | bytes 14155776 | tf_op jit(solution)/shard_map/convert_element_type | solution.py:432
where the time goes:
time: 307 us; the launch traced here: 302 us
  Pallas kernels  248 us (81%)
  matrix products  34.3 us (11%)
  local copies, waits for them, and re-layouts  19.5 us (6%)
    pallas_call x1, Pallas kernels, slab_planes(): pl.pallas_call(slab_kernel, out_shape=jax.ShapeDtypeStruct((planes_rep *...  248 us
    dot_general x1, matrix products, body(): jnp.einsum('pabk,kz->zpba', coefficients, slab_own, preferred_element_typ...  17.5 us
    dot_general x1, matrix products, body(): jnp.einsum('zpba,nz->pabn', plane_grid, slab_back, preferred_element_type...  16.8 us
    convert_element_type x1, local copies, waits for them, and re-layouts, body(): return summed.astype(jnp.bfloat16)  13.9 us

commit v1 on v0

v1 whole, which is shorter than its diff:
```python
import jax
import jax.numpy as jnp
from jax import lax
from jax.experimental import pallas as pl
from jax.experimental.pallas import tpu as pltpu
from jax.sharding import PartitionSpec as P

DAMPING = 0.25
MESH = pl.DeviceIdType.MESH
NT = (((1,), (1,)), ((), ()))


def plain_body(coefficients, noise_field, mode_table):
    rep_index = lax.axis_index("rep")
    col_index = lax.axis_index("my")
    rep_count = lax.axis_size("rep")
    row_count = lax.axis_size("mx")
    col_count = lax.axis_size("my")
    planes_dev = noise_field.shape[0]
    planes_rep = planes_dev * row_count
    planes_all = planes_rep * rep_count
    mode_count = mode_table.shape[0]
    point_count = mode_table.shape[1]
    slab_first = point_count // 2 - planes_all // 2
    row_block = mode_count // row_count
    col_block = mode_count // col_count
    point_block = point_count // col_count
    own_block = mode_count // rep_count
    slab_own = lax.dynamic_slice_in_dim(
        mode_table, slab_first + rep_index * planes_rep, planes_rep, 1
    )
    zmodes = jnp.einsum(
        "pabk,kz->zpba", coefficients, slab_own, preferred_element_type=jnp.float32
    ).astype(jnp.bfloat16)
    zmodes = zmodes.reshape(planes_rep, 2, col_block * row_block)
    spread = lax.all_to_all(zmodes, "mx", split_axis=0, concat_axis=2, tiled=True)
    grouped = spread.reshape(planes_dev, 2, row_count, col_block, row_block)
    tiled_table = mode_table.reshape(row_count, row_block, point_count)
    own_points = lax.dynamic_slice_in_dim(tiled_table, col_index * point_block, point_block, 2)
    block_part = jnp.einsum(
        "zpsal,slx->zpax",
        lax.all_gather(grouped, "my", axis=3, tiled=True),
        own_points,
        preferred_element_type=jnp.float32,
    ).astype(jnp.bfloat16)
    wave_field = jnp.einsum(
        "zpax,ay->zpxy", block_part, mode_table, preferred_element_type=jnp.float32
    )
    wave_real = wave_field[:, 0]
    wave_imag = wave_field[:, 1]
    density = wave_real * wave_real + wave_imag * wave_imag
    noise_wide = noise_field.astype(jnp.float32)
    drive_term = jnp.stack(
        [
            density * (wave_imag - DAMPING * wave_real) + noise_wide[:, 0],
            density * (-wave_real - DAMPING * wave_imag) + noise_wide[:, 1],
        ],
        1,
    ).astype(jnp.bfloat16)
    proj_columns = jnp.einsum(
        "zpxy,ny->zpnx", drive_term, mode_table, preferred_element_type=jnp.float32
    ).astype(jnp.bfloat16)
    block_part = lax.all_to_all(proj_columns, "my", split_axis=2, concat_axis=3, tiled=True)
    folded = jnp.einsum(
        "zpax,slx->zpsal", block_part, tiled_table, preferred_element_type=jnp.float32
    ).astype(jnp.bfloat16)
    proj_rows = folded.reshape(
        block_part.shape[0], block_part.shape[1], row_count * col_block * row_block
    )
    gathered_rows = lax.all_to_all(proj_rows, "mx", split_axis=2, concat_axis=0, tiled=True)
    slab_back = lax.dynamic_slice_in_dim(mode_table, rep_index * own_block, own_block, 0)[
        :, slab_first : slab_first + planes_all
    ]
    portion = lax.all_gather(gathered_rows, "rep", axis=0, tiled=True)
    plane_grid = portion.reshape(portion.shape[0], 2, col_block, row_block)
    summed = jnp.einsum("zpba,nz->pabn", plane_grid, slab_back, preferred_element_type=jnp.float32)
    return summed.astype(jnp.bfloat16)

def slab_schedule(planes, count, units):
    half = count // 2
    per = planes // count

    def first_of(me):
        group = me - half if me >= half else half - 1 - me
        return group * 2 * per + (1 if me >= half else 0)

    def needed(me):
        return max((k + 1) * units - first_of(me) - 2 * k for k in range(per))

    lag_end = max(0, needed(0), needed(count - 1))
    lag_mid = max([lag_end + 1] + [needed(me) for me in range(1, count - 1)])
    return half, per, lag_end, lag_mid


def slab_kernel(own_ref, noise_ref, table_ref, turned_ref, out_ref, modes, lines, total, cubic, parts,
                landed, noise, halves, noise_sem, mode_recv, mode_send, sum_recv, sum_send, last_recv,
                last_send):
    count = lax.axis_size("my")
    me = lax.axis_index("my")
    row_count = lax.axis_size("mx")
    row = lax.axis_index("mx")
    rep_count = lax.axis_size("rep")
    rep = lax.axis_index("rep")
    planes = own_ref.shape[0] // row_count
    block = own_ref.shape[2]
    row_block = own_ref.shape[3]
    offsets = [(dr, dh) for dr in range(rep_count) for dh in range(row_count)]
    mode_count, point_count = table_ref.shape
    point_block = noise_ref.shape[2]
    width = lines.shape[1] // 2
    units = point_count // width
    chunk = 256 if point_count % 256 == 0 else 128
    half, per, lag_end, lag_mid = slab_schedule(planes, count, units)
    up = {"my": me + 1}
    down = {"my": me - 1}
    has_up = me < count - 1
    has_down = me > 0

    barrier = pltpu.get_barrier_semaphore()
    line_peers = [(dh, dm) for dh in range(row_count) for dm in range(count)][1:]
    rep_peers = [(dr, dh) for dr, dh in offsets if dr > 0]
    for dh, dm in line_peers:
        pl.semaphore_signal(
            barrier, inc=1,
            device_id={"mx": lax.rem(row + dh, row_count), "my": lax.rem(me + dm, count)},
            device_id_type=MESH,
        )
    for dr, dh in rep_peers:
        pl.semaphore_signal(
            barrier, inc=1,
            device_id={"rep": lax.rem(rep + dr, rep_count), "mx": lax.rem(row + dh, row_count)},
            device_id_type=MESH,
        )

    def rows(j):
        return pl.ds(pl.multiple_of(j * block, block), block)

    def owner_of(p):
        group = lax.div(p, 2 * per)
        return jnp.where(lax.rem(p, 2) == 1, half + group, half - 1 - group)

    def slot_of(p):
        return lax.div(lax.rem(p, 2 * per), 2)

    def plane_of(k):
        group = jnp.where(me >= half, me - half, half - 1 - me)
        return group * (2 * per) + 2 * k + (me >= half).astype(jnp.int32)

    def mode_copy(p, h, j, target_row, target):
        return pltpu.make_async_remote_copy(
            src_ref=own_ref.at[target_row * planes + p],
            dst_ref=modes.at[slot_of(p), h, :, rows(j)],
            send_sem=mode_send.at[p, target_row],
            recv_sem=mode_recv.at[slot_of(p), h, j],
            device_id={"mx": target_row, "my": target},
            device_id_type=MESH,
        )

    def mode_keep(p):
        return pltpu.make_async_copy(
            own_ref.at[row * planes + p], modes.at[slot_of(p), row, :, rows(me)],
            mode_recv.at[slot_of(p), row, me],
        )

    def last_copy(p, at, received):
        dr, dh = offsets[at]
        target = lax.rem(row + dh, row_count)
        if received:
            from_rep = lax.rem(rep + rep_count - dr, rep_count)
            from_row = lax.rem(row + row_count - dh, row_count)
        else:
            from_rep, from_row = rep, row
        plane = (from_rep * row_count + from_row) * planes + p
        if at == 0:
            return pltpu.make_async_copy(halves.at[p, row], out_ref.at[plane], last_send.at[p, 0])
        return pltpu.make_async_remote_copy(
            src_ref=halves.at[p, target],
            dst_ref=out_ref.at[plane],
            send_sem=last_send.at[p, at],
            recv_sem=last_recv.at[p, at],
            device_id={"rep": lax.rem(rep + dr, rep_count), "mx": target},
            device_id_type=MESH,
        )

    def noise_copy(p):
        slot = lax.rem(p, 2)
        return pltpu.make_async_copy(noise_ref.at[p], noise.at[slot], noise_sem.at[slot])

    def sum_copy(p, j, way, slot):
        return pltpu.make_async_remote_copy(
            src_ref=parts.at[p, :, rows(j)],
            dst_ref=landed.at[p, slot],
            send_sem=sum_send.at[p, way, j],
            recv_sem=sum_recv.at[p, slot],
            device_id=down if way else up,
            device_id_type=MESH,
        )

    noise_copy(0).start()
    if planes > 1:
        noise_copy(1).start()

    pl.semaphore_wait(barrier, len(line_peers) + len(rep_peers))

    def send_modes(p, carry):
        target = owner_of(p)
        for dh in range(row_count):
            target_row = lax.rem(row + dh, row_count)
            if dh:
                mode_copy(p, row, me, target_row, target).start()
            else:
                @pl.when(target != me)
                def _():
                    mode_copy(p, row, me, target_row, target).start()

                @pl.when(target == me)
                def _():
                    mode_keep(p).start()
        return carry

    lax.fori_loop(0, planes, send_modes, 0)

    def inside(p):
        return jnp.logical_and(p >= 0, p < planes)

    own_points = pl.ds(pl.multiple_of(me * point_block, point_block), point_block)

    def project_noise(p):
        noise_copy(p).wait()
        slot = lax.rem(p, 2)
        step_of = max(c for c in (512, 256, 128) if point_count % c == 0)
        columns = None
        for first in range(0, point_count, step_of):
            span = slice(first, first + step_of)
            field = noise[slot, :, :, span].reshape(2 * point_block, step_of)
            more = lax.dot_general(table_ref[:, span], field, NT, preferred_element_type=jnp.float32)
            columns = more if columns is None else columns + more
        turned = turned_ref[own_points]
        for part in range(2):
            column = columns[:, part * point_block : (part + 1) * point_block].astype(jnp.bfloat16)
            parts[p, part] = jnp.dot(column, turned, preferred_element_type=jnp.float32).astype(
                jnp.bfloat16
            )

        @pl.when(p + 2 < planes)
        def _():
            noise_copy(p + 2).start()

    def wait_modes(k):
        p = plane_of(k)
        for h in range(row_count):
            for j in range(count):
                mine = jnp.logical_and(row == h, me == j)

                @pl.when(mine)
                def _():
                    mode_keep(p).wait()

                @pl.when(jnp.logical_not(mine))
                def _():
                    mode_copy(p, h, j, row, me).wait_recv()

    def cubic_unit(u):
        k = lax.div(u, units)
        at = lax.rem(u, units)

        @pl.when(at == 0)
        def _():
            wait_modes(k)

        span = pl.ds(pl.multiple_of(at * width, width), width)
        for part in range(2):
            line = None
            for h in range(row_count):
                more = jnp.dot(
                    modes[k, h, part], table_ref[h * row_block : (h + 1) * row_block, span],
                    preferred_element_type=jnp.float32,
                )
                line = more if line is None else line + more
            lines[:, part * width : (part + 1) * width] = line.astype(jnp.bfloat16)
        columns = None
        for first in range(0, point_count, chunk):
            wave = jnp.dot(
                turned_ref[first : first + chunk], lines[...], preferred_element_type=jnp.float32
            )
            wave_real, wave_imag = wave[:, :width], wave[:, width:]
            density = wave_real * wave_real + wave_imag * wave_imag
            drive = jnp.concatenate(
                [
                    (density * (wave_imag - DAMPING * wave_real)).astype(jnp.bfloat16),
                    (density * (-wave_real - DAMPING * wave_imag)).astype(jnp.bfloat16),
                ],
                1,
            )
            more = jnp.dot(
                table_ref[:, first : first + chunk], drive, preferred_element_type=jnp.float32
            )
            columns = more if columns is None else columns + more
        for part in range(2):
            more = jnp.dot(
                columns[:, part * width : (part + 1) * width].astype(jnp.bfloat16),
                turned_ref[span], preferred_element_type=jnp.float32,
            )

            @pl.when(at == 0)
            def _():
                total[part] = more

            @pl.when(at > 0)
            def _():
                total[part] += more

        @pl.when(at == units - 1)
        def _():
            cubic[k] = total[...].astype(jnp.bfloat16)

    def add(p, j, slot):
        wide = parts[p, :, rows(j)].astype(jnp.float32) + landed[p, slot].astype(jnp.float32)
        parts[p, :, rows(j)] = wide.astype(jnp.bfloat16)

    rise_lag = jnp.where(me == 0, lag_end, lag_mid + me - 1)
    sink_lag = jnp.where(me == count - 1, lag_end, lag_mid + count - 2 - me)
    merge_lag = jnp.minimum(rise_lag, sink_lag)
    done_lag = jnp.maximum(rise_lag, sink_lag)

    def step(s, carry):
        @pl.when(s < planes)
        def _():
            project_noise(s)

        merging = s - merge_lag

        @pl.when(jnp.logical_and(inside(merging), owner_of(merging) == me))
        def _():
            wide = parts[merging].astype(jnp.float32) + cubic[slot_of(merging)].astype(jnp.float32)
            parts[merging] = wide.astype(jnp.bfloat16)

        rising = s - rise_lag
        sinking = s - sink_lag

        @pl.when(jnp.logical_and(inside(rising), me == 0))
        def _():
            for j in range(count - 1, 0, -1):
                sum_copy(rising, j, 0, j).start()

        @pl.when(jnp.logical_and(inside(sinking), me == count - 1))
        def _():
            for j in range(count - 1):
                sum_copy(sinking, j, 1, count if j == count - 2 else j).start()

        @pl.when(s < per * units)
        def _():
            cubic_unit(s)

        for far in range(count - 2, 0, -1):
            @pl.when(jnp.logical_and(jnp.logical_and(inside(rising), has_down), me + far <= count - 1))
            def _():
                j = me + far
                sum_copy(rising, j, 0, j).wait_recv()
                add(rising, j, j)
                sum_copy(rising, j, 0, j).start()

        for far in range(count - 2, 0, -1):
            @pl.when(jnp.logical_and(jnp.logical_and(inside(sinking), has_up), me - far >= 0))
            def _():
                j = me - far
                sum_copy(sinking, j, 1, j).wait_recv()
                add(sinking, j, j)
                sum_copy(sinking, j, 1, count if far == 1 else j).start()

        done = s - done_lag

        @pl.when(inside(done))
        def _():
            @pl.when(has_down)
            def _():
                sum_copy(done, me, 0, me).wait_recv()
                add(done, me, me)

            @pl.when(has_up)
            def _():
                sum_copy(done, me, 1, count).wait_recv()
                add(done, me, count)

            for part in range(2):
                whole = parts[done, part, rows(me)]
                for h in range(row_count):
                    halves[done, h, part] = whole[:, h * row_block : (h + 1) * row_block]
            for at in range(len(offsets)):
                last_copy(done, at, False).start()

        return carry

    lax.fori_loop(0, planes + lag_mid + count - 2, step, 0)

    def finish(p, carry):
        for j in range(count):
            @pl.when(j > me)
            def _():
                sum_copy(p, j, 0, j).wait_send()

            @pl.when(j < me)
            def _():
                sum_copy(p, j, 1, j).wait_send()

        target = owner_of(p)
        for dh in range(row_count):
            target_row = lax.rem(row + dh, row_count)
            if dh:
                mode_copy(p, row, me, target_row, target).wait_send()
            else:
                @pl.when(target != me)
                def _():
                    mode_copy(p, row, me, target_row, target).wait_send()

        last_copy(p, 0, False).wait()
        for at in range(1, len(offsets)):
            last_copy(p, at, False).wait_send()
            last_copy(p, at, True).wait_recv()
        return carry

    lax.fori_loop(0, planes, finish, 0)


def slab_planes(own_modes, noise_field, mode_table, turned):
    count = lax.axis_size("my")
    mode_count = mode_table.shape[0]
    row_count = lax.axis_size("mx")
    rep_count = lax.axis_size("rep")
    planes_rep, _, block, row_block = own_modes.shape
    planes = planes_rep // row_count
    per = planes // count
    point_block, point_count = noise_field.shape[2:]
    width = max(c for c in (512, 256, 128) if point_count % c == 0)
    vmem = pl.BlockSpec(memory_space=pltpu.VMEM)
    hbm = pl.BlockSpec(memory_space=pl.ANY)
    dma = pltpu.SemaphoreType.DMA
    flops = 12 * planes * mode_count * point_block * (point_count + mode_count)
    return pl.pallas_call(
        slab_kernel,
        out_shape=jax.ShapeDtypeStruct((planes_rep * rep_count, 2, block, row_block), jnp.bfloat16),
        in_specs=[hbm, hbm, vmem, vmem],
        out_specs=hbm,
        scratch_shapes=[
            pltpu.VMEM((per, row_count, 2, mode_count, row_block), jnp.bfloat16),
            pltpu.VMEM((mode_count, 2 * width), jnp.bfloat16),
            pltpu.VMEM((2, mode_count, mode_count), jnp.float32),
            pltpu.VMEM((per, 2, mode_count, mode_count), jnp.bfloat16),
            pltpu.VMEM((planes, 2, mode_count, mode_count), jnp.bfloat16),
            pltpu.VMEM((planes, count + 1, 2, block, mode_count), jnp.bfloat16),
            pltpu.VMEM((2, 2, point_block, point_count), jnp.bfloat16),
            pltpu.VMEM((planes, row_count, 2, block, row_block), jnp.bfloat16),
            dma((2,)),
            dma((per, row_count, count)),
            dma((planes, row_count)),
            dma((planes, count + 1)),
            dma((planes, 2, count)),
            dma((planes, row_count * rep_count)),
            dma((planes, row_count * rep_count)),
        ],
        compiler_params=pltpu.CompilerParams(
            collective_id=0, has_side_effects=True, vmem_limit_bytes=60 * 1024 * 1024
        ),
        cost_estimate=pl.CostEstimate(
            flops=flops, bytes_accessed=noise_field.size * 2, transcendentals=0
        ),
    )(own_modes, noise_field, mode_table, turned)


def body(coefficients, noise_field, mode_table):
    rep_index = lax.axis_index("rep")
    rep_count = lax.axis_size("rep")
    row_count = lax.axis_size("mx")
    col_count = lax.axis_size("my")
    planes_dev = noise_field.shape[0]
    planes_rep = planes_dev * row_count
    planes_all = planes_rep * rep_count
    mode_count = mode_table.shape[0]
    point_count = mode_table.shape[1]
    slab_first = point_count // 2 - planes_all // 2
    row_block = mode_count // row_count
    col_block = mode_count // col_count
    point_block = point_count // col_count
    own_block = mode_count // rep_count
    if (
        col_block % 16 or row_block % 16 or point_block % 128 or mode_count % 128
        or col_count < 2 or col_count % 2 or planes_dev % col_count
    ):
        return plain_body(coefficients, noise_field, mode_table)
    slab_own = lax.dynamic_slice_in_dim(
        mode_table, slab_first + rep_index * planes_rep, planes_rep, 1
    )
    zmodes = jnp.einsum(
        "pabk,kz->zpba", coefficients, slab_own, preferred_element_type=jnp.float32
    ).astype(jnp.bfloat16)
    plane_grid = slab_planes(zmodes, noise_field, mode_table, mode_table.T)
    slab_back = lax.dynamic_slice_in_dim(mode_table, rep_index * own_block, own_block, 0)[
        :, slab_first : slab_first + planes_all
    ]
    summed = jnp.einsum("zpba,nz->pabn", plane_grid, slab_back, preferred_element_type=jnp.float32)
    return summed.astype(jnp.bfloat16)


def solution(mesh):
    in_specs = (P(None, "mx", "my", None), P(("rep", "mx"), None, "my", None), P())
    out_specs = P(None, "mx", "my", "rep")
    return jax.shard_map(body, mesh=mesh, in_specs=in_specs, out_specs=out_specs, check_vma=False)
```

time: 307 us -> 323 us (1.052)
  Pallas kernels: 248 us -> 267 us
    pallas_call x1, Pallas kernels: 248 us -> 267 us  [slab_planes(): pl.pallas_call(slab_kernel, out_shape=jax.ShapeDtypeStruct((planes_rep *...]
where the time goes in v1:
time: 323 us; the launch traced here: 321 us
  Pallas kernels  267 us (83%)
  matrix products  34.3 us (11%)
  local copies, waits for them, and re-layouts  20 us (6%)
    pallas_call x1, Pallas kernels, slab_planes(): pl.pallas_call(slab_kernel, out_shape=jax.ShapeDtypeStruct((planes_rep *...  267 us
    dot_general x1, matrix products, body(): jnp.einsum('pabk,kz->zpba', coefficients, slab_own, preferred_element_typ...  17.5 us
    dot_general x1, matrix products, body(): jnp.einsum('zpba,nz->pabn', plane_grid, slab_back, preferred_element_type...  16.8 us
    convert_element_type x1, local copies, waits for them, and re-layouts, body(): return summed.astype(jnp.bfloat16)  13.9 us

profile of v1, /device:TPU:0, one launch (start us, length us, event | category | flops | bytes accessed | tf_op | source)
XLA Modules:
  0.0 321.1 jit_solution(9431180672789097680)
XLA Ops:
  0.0 2.4 copy.4
  2.4 17.5 %fusion.4 = bf16[32,2,192,96]{3,0,2,1:T(8,128)(2,1)S(1)} fusion(bf16[2,192,96,384]{3,2,1,0:T(8,128)(2,1)} %param.3, bf16[384,1536]{1,0:T(8,128)(2,1)} %table_ref.1, s32[]{:T(128)S(6)} %select_n.7), kind=kOutput, calls=%fused_computation.4 | convolution fusion | flops 905969664 | bytes 30769156 | tf_op jit(solution)/shard_map/pabk,kz->zpba/dot_general | solution.py:493
  19.9 3.8 %copy.8 = bf16[32,2,192,96]{2,3,1,0:T(8,128)(2,1)} copy(bf16[32,2,192,96]{3,0,2,1:T(8,128)(2,1)S(1)} %fusion.4) | data formatting | bytes 4718592 | tf_op jit(solution)/shard_map/pabk,kz->zpba/dot_general | solution.py:493
  23.7 266.7 %shard_map.37 = bf16[128,2,96,192]{3,2,1,0:T(8,128)(2,1)} custom-call(bf16[32,2,96,192]{3,2,1,0:T(8,128)(2,1)} %bitcast.17, bf16[16,2,384,1536]{3,2,1,0:T(8,128)(2,1)} %noise_ref.1, bf16[384,1536]{1,0:T(8,128)(2,1)} %table_ref.1, bf16[1536,384]{1,0:T(8,128)(2,1)} %bitcast.18), custom_call_target="tpu_custom_call" | custom-call | flops 54358179840 | bytes 37748736 | tf_op jit(solution)/shard_map/pallas_call | solution.py:439
  290.4 16.8 %convert_bitcast_fusion = bf16[2,192,96,96]{1,3,2,0:T(8,128)(2,1)} fusion(bf16[128,2,96,192]{3,2,1,0:T(8,128)(2,1)} %shard_map.37, bf16[384,1536]{1,0:T(8,128)(2,1)} %table_ref.1, s32[]{:T(128)S(6)} %select_n.6, s32[]{:T(128)S(6)} %add.10), kind=kOutput, calls=%fused_computation.2 | convolution fusion | flops 909508608 | bytes 19685384 | tf_op jit(solution)/shard_map/zpba,nz->pabn/dot_general | solution.py:500
  307.2 13.9 %copy.6 = bf16[2,192,96,96]{3,2,1,0:T(8,128)(2,1)} copy(bf16[2,192,96,96]{1,3,2,0:T(8,128)(2,1)} %convert_bitcast_fusion) | data formatting | bytes 14155776 | tf_op jit(solution)/shard_map/convert_element_type | solution.py:501

commit v2 on v1

--- a/solution.py
+++ b/solution.py
@@ -76,7 +76,7 @@
     summed = jnp.einsum("zpba,nz->pabn", plane_grid, slab_back, preferred_element_type=jnp.float32)
     return summed.astype(jnp.bfloat16)
 
-def slab_schedule(planes, count, units):
+def slab_schedule(planes, count, units, rate, first_step):
     half = count // 2
     per = planes // count
 
@@ -85,32 +85,42 @@
         return group * 2 * per + (1 if me >= half else 0)
 
     def needed(me):
-        return max((k + 1) * units - first_of(me) - 2 * k for k in range(per))
+        ready = [first_step + ((k + 1) * units - 1) // rate for k in range(per)]
+        return max(ready[k] + 1 - first_of(me) - 2 * k for k in range(per))
 
     lag_end = max(0, needed(0), needed(count - 1))
     lag_mid = max([lag_end + 1] + [needed(me) for me in range(1, count - 1)])
     return half, per, lag_end, lag_mid
 
 
-def slab_kernel(own_ref, noise_ref, table_ref, turned_ref, out_ref, modes, lines, total, cubic, parts,
-                landed, noise, halves, noise_sem, mode_recv, mode_send, sum_recv, sum_send, last_recv,
-                last_send):
+def slab_kernel(coef_ref, noise_ref, table_ref, turned_ref, slab_ref, out_ref, coef, wide, spread, zmodes,
+                modes, lines, total, cubic, parts, landed, noise, halves, coef_sem, noise_sem, mode_recv,
+                mode_send, sum_recv, sum_send, first_recv, first_send, second_recv, second_send):
     count = lax.axis_size("my")
     me = lax.axis_index("my")
     row_count = lax.axis_size("mx")
     row = lax.axis_index("mx")
     rep_count = lax.axis_size("rep")
     rep = lax.axis_index("rep")
-    planes = own_ref.shape[0] // row_count
-    block = own_ref.shape[2]
-    row_block = own_ref.shape[3]
+    planes = noise_ref.shape[0]
+    planes_rep = planes * row_count
+    row_block = coef_ref.shape[1]
+    block = coef_ref.shape[2]
+    pair = 2 if rep_count % 2 == 0 else 1
+    groups = rep_count // pair
+    group = lax.div(rep, pair)
+    side = lax.rem(rep, pair)
+    spots = [(dg, dh) for dg in range(groups) for dh in range(row_count)]
     offsets = [(dr, dh) for dr in range(rep_count) for dh in range(row_count)]
+    tiles = [(t, first, min(128, row_block - first)) for t, first in enumerate(range(0, row_block, 128))]
     mode_count, point_count = table_ref.shape
     point_block = noise_ref.shape[2]
     width = lines.shape[1] // 2
     units = point_count // width
     chunk = 256 if point_count % 256 == 0 else 128
-    half, per, lag_end, lag_mid = slab_schedule(planes, count, units)
+    rate = max(1, units // 2)
+    modes_step, cubic_step = 2, 4
+    half, per, lag_end, lag_mid = slab_schedule(planes, count, units, rate, cubic_step)
     up = {"my": me + 1}
     down = {"my": me - 1}
     has_up = me < count - 1
@@ -148,7 +158,7 @@
 
     def mode_copy(p, h, j, target_row, target):
         return pltpu.make_async_remote_copy(
-            src_ref=own_ref.at[target_row * planes + p],
+            src_ref=zmodes.at[target_row * planes + p],
             dst_ref=modes.at[slot_of(p), h, :, rows(j)],
             send_sem=mode_send.at[p, target_row],
             recv_sem=mode_recv.at[slot_of(p), h, j],
@@ -158,27 +168,47 @@
 
     def mode_keep(p):
         return pltpu.make_async_copy(
-            own_ref.at[row * planes + p], modes.at[slot_of(p), row, :, rows(me)],
+            zmodes.at[row * planes + p], modes.at[slot_of(p), row, :, rows(me)],
             mode_recv.at[slot_of(p), row, me],
         )
 
-    def last_copy(p, at, received):
-        dr, dh = offsets[at]
-        target = lax.rem(row + dh, row_count)
+    def plane_at(from_group, from_side, from_row, p):
+        return ((from_group * pair + from_side) * row_count + from_row) * planes + p
+
+    def first_copy(p, at, received):
+        dg, dh = spots[at]
+        target_row = lax.rem(row + dh, row_count)
+        if at == 0:
+            return pltpu.make_async_copy(
+                halves.at[p, row], out_ref.at[plane_at(group, side, row, p)], first_send.at[p, 0]
+            )
         if received:
-            from_rep = lax.rem(rep + rep_count - dr, rep_count)
-            from_row = lax.rem(row + row_count - dh, row_count)
+            plane = plane_at(
+                lax.rem(group + groups - dg, groups), side, lax.rem(row + row_count - dh, row_count), p
+            )
         else:
-            from_rep, from_row = rep, row
-        plane = (from_rep * row_count + from_row) * planes + p
-        if at == 0:
-            return pltpu.make_async_copy(halves.at[p, row], out_ref.at[plane], last_send.at[p, 0])
+            plane = plane_at(group, side, row, p)
         return pltpu.make_async_remote_copy(
-            src_ref=halves.at[p, target],
+            src_ref=halves.at[p, target_row],
             dst_ref=out_ref.at[plane],
-            send_sem=last_send.at[p, at],
-            recv_sem=last_recv.at[p, at],
-            device_id={"rep": lax.rem(rep + dr, rep_count), "mx": target},
+            send_sem=first_send.at[p, at],
+            recv_sem=first_recv.at[p, at],
+            device_id={"rep": lax.rem(group + dg, groups) * pair + side, "mx": target_row},
+            device_id_type=MESH,
+        )
+
+    def second_copy(p, at, received):
+        dg, dh = spots[at]
+        plane = plane_at(
+            lax.rem(group + groups - dg, groups), 1 - side if received else side,
+            lax.rem(row + row_count - dh, row_count), p,
+        )
+        return pltpu.make_async_remote_copy(
+            src_ref=halves.at[p, row] if at == 0 else out_ref.at[plane],
+            dst_ref=out_ref.at[plane],
+            send_sem=second_send.at[p, at],
+            recv_sem=second_recv.at[p, at],
+            device_id={"rep": group * pair + 1 - side},
             device_id_type=MESH,
         )
 
@@ -196,11 +226,47 @@
             device_id_type=MESH,
         )
 
+    strips = block // 16
+
+    def coef_copy(i):
+        slot = lax.rem(i, 2)
+        strip = pl.ds(pl.multiple_of(lax.rem(i, strips) * 16, 16), 16)
+        return pltpu.make_async_copy(
+            coef_ref.at[lax.div(i, strips), :, strip], coef.at[slot], coef_sem.at[slot]
+        )
+
     noise_copy(0).start()
     if planes > 1:
         noise_copy(1).start()
+    coef_copy(0).start()
+    coef_copy(1).start()
 
     pl.semaphore_wait(barrier, len(line_peers) + len(rep_peers))
+
+    def contract_strip(i, carry):
+        coef_copy(i).wait()
+        part = lax.div(i, strips)
+        strip = pl.ds(pl.multiple_of(lax.rem(i, strips) * 16, 16), 16)
+        wide[...] = jnp.dot(
+            coef[lax.rem(i, 2)].reshape(row_block * 16, coef.shape[3]), slab_ref[...],
+            preferred_element_type=jnp.float32,
+        )
+
+        @pl.when(i + 2 < 2 * strips)
+        def _():
+            coef_copy(i + 2).start()
+
+        for b in range(16):
+            for t, first, size in tiles:
+                turn = wide[pl.ds(first * 16 + b, size, stride=16), :].T[:planes_rep]
+                if size < 128:
+                    turn = jnp.concatenate([turn, jnp.zeros((planes_rep, 128 - size), jnp.float32)], 1)
+                spread[t, pl.ds(b, planes_rep, stride=16), :] = turn
+        for t, first, size in tiles:
+            zmodes[:, part, strip, first : first + size] = (
+                spread[t, :, :size].reshape(planes_rep, 16, size).astype(jnp.bfloat16)
+            )
+        return carry
 
     def send_modes(p, carry):
         target = owner_of(p)
@@ -217,8 +283,6 @@
                 def _():
                     mode_keep(p).start()
         return carry
-
-    lax.fori_loop(0, planes, send_modes, 0)
 
     def inside(p):
         return jnp.logical_and(p >= 0, p < planes)
@@ -260,7 +324,7 @@
                 def _():
                     mode_copy(p, h, j, row, me).wait_recv()
 
-    def cubic_unit(u):
+    def cubic_unit(u, carry):
         k = lax.div(u, units)
         at = lax.rem(u, units)
 
@@ -314,9 +378,11 @@
         def _():
             cubic[k] = total[...].astype(jnp.bfloat16)
 
+        return carry
+
     def add(p, j, slot):
-        wide = parts[p, :, rows(j)].astype(jnp.float32) + landed[p, slot].astype(jnp.float32)
-        parts[p, :, rows(j)] = wide.astype(jnp.bfloat16)
+        both = parts[p, :, rows(j)].astype(jnp.float32) + landed[p, slot].astype(jnp.float32)
+        parts[p, :, rows(j)] = both.astype(jnp.bfloat16)
 
     rise_lag = jnp.where(me == 0, lag_end, lag_mid + me - 1)
     sink_lag = jnp.where(me == count - 1, lag_end, lag_mid + count - 2 - me)
@@ -332,8 +398,8 @@
 
         @pl.when(jnp.logical_and(inside(merging), owner_of(merging) == me))
         def _():
-            wide = parts[merging].astype(jnp.float32) + cubic[slot_of(merging)].astype(jnp.float32)
-            parts[merging] = wide.astype(jnp.bfloat16)
+            both = parts[merging].astype(jnp.float32) + cubic[slot_of(merging)].astype(jnp.float32)
+            parts[merging] = both.astype(jnp.bfloat16)
 
         rising = s - rise_lag
         sinking = s - sink_lag
@@ -348,9 +414,15 @@
             for j in range(count - 1):
                 sum_copy(sinking, j, 1, count if j == count - 2 else j).start()
 
-        @pl.when(s < per * units)
-        def _():
-            cubic_unit(s)
+        @pl.when(s == modes_step)
+        def _():
+            lax.fori_loop(0, 2 * strips, contract_strip, 0)
+            lax.fori_loop(0, planes, send_modes, 0)
+
+        unit = (s - cubic_step) * rate
+        lax.fori_loop(
+            jnp.clip(unit, 0, per * units), jnp.clip(unit + rate, 0, per * units), cubic_unit, 0
+        )
 
         for far in range(count - 2, 0, -1):
             @pl.when(jnp.logical_and(jnp.logical_and(inside(rising), has_down), me + far <= count - 1))
@@ -386,12 +458,23 @@
                 whole = parts[done, part, rows(me)]
                 for h in range(row_count):
                     halves[done, h, part] = whole[:, h * row_block : (h + 1) * row_block]
-            for at in range(len(offsets)):
-                last_copy(done, at, False).start()
+            for at in range(len(spots) - 1, -1, -1):
+                first_copy(done, at, False).start()
+            if pair == 2:
+                second_copy(done, 0, False).start()
+
+        passing = done - 1
+
+        @pl.when(inside(passing))
+        def _():
+            for at in range(1, len(spots)):
+                first_copy(passing, at, True).wait_recv()
+                if pair == 2:
+                    second_copy(passing, at, False).start()
 
         return carry
 
-    lax.fori_loop(0, planes + lag_mid + count - 2, step, 0)
+    lax.fori_loop(0, planes + lag_mid + count - 1, step, 0)
 
     def finish(p, carry):
         for j in range(count):
@@ -413,25 +496,31 @@
                 def _():
                     mode_copy(p, row, me, target_row, target).wait_send()
 
-        last_copy(p, 0, False).wait()
-        for at in range(1, len(offsets)):
-            last_copy(p, at, False).wait_send()
-            last_copy(p, at, True).wait_recv()
+        first_copy(p, 0, False).wait()
+        for at in range(len(spots)):
+            if at:
+                first_copy(p, at, False).wait_send()
+            if pair == 2:
+                second_copy(p, at, False).wait_send()
+                second_copy(p, at, True).wait_recv()
         return carry
 
     lax.fori_loop(0, planes, finish, 0)
 
 
-def slab_planes(own_modes, noise_field, mode_table, turned):
+def slab_planes(coefficients, noise_field, mode_table, turned, slab_own):
     count = lax.axis_size("my")
     mode_count = mode_table.shape[0]
     row_count = lax.axis_size("mx")
     rep_count = lax.axis_size("rep")
-    planes_rep, _, block, row_block = own_modes.shape
-    planes = planes_rep // row_count
+    _, row_block, block, depth = coefficients.shape
+    planes = noise_field.shape[0]
+    planes_rep = planes * row_count
     per = planes // count
+    spots = row_count * (rep_count // (2 if rep_count % 2 == 0 else 1))
     point_block, point_count = noise_field.shape[2:]
-    width = max(c for c in (512, 256, 128) if point_count % c == 0)
+    width = max(c for c in (256, 128) if point_count % c == 0)
+    lanes = slab_own.shape[1]
     vmem = pl.BlockSpec(memory_space=pltpu.VMEM)
     hbm = pl.BlockSpec(memory_space=pl.ANY)
     dma = pltpu.SemaphoreType.DMA
@@ -439,9 +528,13 @@
     return pl.pallas_call(
         slab_kernel,
         out_shape=jax.ShapeDtypeStruct((planes_rep * rep_count, 2, block, row_block), jnp.bfloat16),
-        in_specs=[hbm, hbm, vmem, vmem],
+        in_specs=[hbm, hbm, vmem, vmem, vmem],
         out_specs=hbm,
         scratch_shapes=[
+            pltpu.VMEM((2, row_block, 16, depth), jnp.bfloat16),
+            pltpu.VMEM((row_block * 16, lanes), jnp.float32),
+            pltpu.VMEM((pl.cdiv(row_block, 128), planes_rep * 16, 128), jnp.float32),
+            pltpu.VMEM((planes_rep, 2, block, row_block), jnp.bfloat16),
             pltpu.VMEM((per, row_count, 2, mode_count, row_block), jnp.bfloat16),
             pltpu.VMEM((mode_count, 2 * width), jnp.bfloat16),
             pltpu.VMEM((2, mode_count, mode_count), jnp.float32),
@@ -451,12 +544,15 @@
             pltpu.VMEM((2, 2, point_block, point_count), jnp.bfloat16),
             pltpu.VMEM((planes, row_count, 2, block, row_block), jnp.bfloat16),
             dma((2,)),
+            dma((2,)),
             dma((per, row_count, count)),
             dma((planes, row_count)),
             dma((planes, count + 1)),
             dma((planes, 2, count)),
-            dma((planes, row_count * rep_count)),
-            dma((planes, row_count * rep_count)),
+            dma((planes, spots)),
+            dma((planes, spots)),
+            dma((planes, spots)),
+            dma((planes, spots)),
         ],
         compiler_params=pltpu.CompilerParams(
             collective_id=0, has_side_effects=True, vmem_limit_bytes=60 * 1024 * 1024
@@ -464,7 +560,7 @@
         cost_estimate=pl.CostEstimate(
             flops=flops, bytes_accessed=noise_field.size * 2, transcendentals=0
         ),
-    )(own_modes, noise_field, mode_table, turned)
+    )(coefficients, noise_field, mode_table, turned, slab_own)
 
 
 def body(coefficients, noise_field, mode_table):
@@ -484,16 +580,14 @@
     own_block = mode_count // rep_count
     if (
         col_block % 16 or row_block % 16 or point_block % 128 or mode_count % 128
-        or col_count < 2 or col_count % 2 or planes_dev % col_count
+        or col_count < 2 or col_count % 2 or planes_dev % col_count or planes_rep > 128 or planes_rep % 8
     ):
         return plain_body(coefficients, noise_field, mode_table)
     slab_own = lax.dynamic_slice_in_dim(
         mode_table, slab_first + rep_index * planes_rep, planes_rep, 1
     )
-    zmodes = jnp.einsum(
-        "pabk,kz->zpba", coefficients, slab_own, preferred_element_type=jnp.float32
-    ).astype(jnp.bfloat16)
-    plane_grid = slab_planes(zmodes, noise_field, mode_table, mode_table.T)
+    slab_own = jnp.pad(slab_own, ((0, 0), (0, 128 - planes_rep)))
+    plane_grid = slab_planes(coefficients, noise_field, mode_table, mode_table.T, slab_own)
     slab_back = lax.dynamic_slice_in_dim(mode_table, rep_index * own_block, own_block, 0)[
         :, slab_first : slab_first + planes_all
     ]

time: 323 us -> 274 us (0.85)
  Pallas kernels: 267 us -> 239 us
  matrix products: 34.3 us -> 16.8 us
    pallas_call x1, Pallas kernels: 267 us -> 239 us  [slab_planes(): pl.pallas_call(slab_kernel, out_shape=jax.ShapeDtypeStruct((planes_rep *...]
    dot_general x1 -> x0, matrix products: 17.5 us -> none  [body(): jnp.einsum('pabk,kz->zpba', coefficients, slab_own, preferred_element_typ...]
    dot_general x1 -> x0, local copies, waits for them, and re-layouts: 3.75 us -> none  [body(): jnp.einsum('pabk,kz->zpba', coefficients, slab_own, preferred_element_typ...]
where the time goes in v2:
time: 274 us
  Pallas kernels  239 us (87%)
  local copies, waits for them, and re-layouts  17.9 us (7%)
  matrix products  16.8 us (6%)
    pallas_call x1, Pallas kernels, slab_planes(): pl.pallas_call(slab_kernel, out_shape=jax.ShapeDtypeStruct((planes_rep *...  239 us
    dot_general x1, matrix products, body(): jnp.einsum('zpba,nz->pabn', plane_grid, slab_back, preferred_element_type...  16.8 us
    convert_element_type x1, local copies, waits for them, and re-layouts, body(): return summed.astype(jnp.bfloat16)  13.9 us

profile of v2, /device:TPU:0, one launch (start us, length us, event | category | flops | bytes accessed | tf_op | source)
XLA Modules:
  0.0 273.8 jit_solution(2831088375534406638)
XLA Ops:
  0.0 1.0 constant_dynamic-slice_fusion
  1.0 0.7 pad.4.slab_ref
  1.7 2.4 copy.4
  4.0 239.1 %shard_map.37 = bf16[128,2,96,192]{3,2,1,0:T(8,128)(2,1)} custom-call(bf16[2,192,96,384]{3,2,1,0:T(8,128)(2,1)} %coef_ref.1, bf16[16,2,384,1536]{3,2,1,0:T(8,128)(2,1)} %noise_ref.1, bf16[384,1536]{1,0:T(8,128)(2,1)} %table_ref.1, bf16[1536,384]{1,0:T(8,128)(2,1)} %bitcast.8, bf16[384,128]{1,0:T(8,128)(2,1)} %pad.4.slab_ref), custom_call_target="tpu_custom_call" | custom-call | flops 54358179840 | bytes 37748736 | tf_op jit(solution)/shard_map/pallas_call | solution.py:528
  243.1 16.8 %convert_bitcast_fusion = bf16[2,192,96,96]{1,3,2,0:T(8,128)(2,1)} fusion(bf16[128,2,96,192]{3,2,1,0:T(8,128)(2,1)} %shard_map.37, bf16[384,1536]{1,0:T(8,128)(2,1)} %table_ref.1, s32[]{:T(128)S(6)} %select_n.6, s32[]{:T(128)S(6)} %add.12), kind=kOutput, calls=%fused_computation.2 | convolution fusion | flops 909508608 | bytes 19685384 | tf_op jit(solution)/shard_map/zpba,nz->pabn/dot_general | solution.py:594
  260.0 13.9 %copy.6 = bf16[2,192,96,96]{3,2,1,0:T(8,128)(2,1)} copy(bf16[2,192,96,96]{1,3,2,0:T(8,128)(2,1)} %convert_bitcast_fusion) | data formatting | bytes 14155776 | tf_op jit(solution)/shard_map/convert_element_type | solution.py:595

commit v3 on v2

--- a/solution.py
+++ b/solution.py
@@ -76,25 +76,30 @@
     summed = jnp.einsum("zpba,nz->pabn", plane_grid, slab_back, preferred_element_type=jnp.float32)
     return summed.astype(jnp.bfloat16)
 
+def slab_owners(planes, count):
+    half = count // 2
+    inner = max(1, planes // count // 2)
+    shared = 2 * inner * (half - 1)
+    return half, inner, shared, (planes - shared) // 2
+
+
 def slab_schedule(planes, count, units, rate, first_step):
-    half = count // 2
-    per = planes // count
-
-    def first_of(me):
+    half, inner, shared, outer = slab_owners(planes, count)
+
+    def needed(me):
         group = me - half if me >= half else half - 1 - me
-        return group * 2 * per + (1 if me >= half else 0)
-
-    def needed(me):
-        ready = [first_step + ((k + 1) * units - 1) // rate for k in range(per)]
-        return max(ready[k] + 1 - first_of(me) - 2 * k for k in range(per))
+        owned = inner if group < half - 1 else outer
+        first = group * 2 * inner + (1 if me >= half else 0)
+        ready = [first_step + ((k + 1) * units - 1) // rate for k in range(owned)]
+        return max(ready[k] + 1 - first - 2 * k for k in range(owned))
 
     lag_end = max(0, needed(0), needed(count - 1))
     lag_mid = max([lag_end + 1] + [needed(me) for me in range(1, count - 1)])
-    return half, per, lag_end, lag_mid
+    return lag_end, lag_mid
 
 
 def slab_kernel(coef_ref, noise_ref, table_ref, turned_ref, slab_ref, out_ref, coef, wide, spread, zmodes,
-                modes, lines, total, cubic, parts, landed, noise, halves, coef_sem, noise_sem, mode_recv,
+                modes, split, lines, total, cubic, parts, landed, noise, halves, coef_sem, noise_sem, mode_recv,
                 mode_send, sum_recv, sum_send, first_recv, first_send, second_recv, second_send):
     count = lax.axis_size("my")
     me = lax.axis_index("my")
@@ -112,7 +117,9 @@
     side = lax.rem(rep, pair)
     spots = [(dg, dh) for dg in range(groups) for dh in range(row_count)]
     offsets = [(dr, dh) for dr in range(rep_count) for dh in range(row_count)]
-    tiles = [(t, first, min(128, row_block - first)) for t, first in enumerate(range(0, row_block, 128))]
+    full = row_block // 128
+    rest = row_block % 128
+    pieces = zmodes.shape[1]
     mode_count, point_count = table_ref.shape
     point_block = noise_ref.shape[2]
     width = lines.shape[1] // 2
@@ -120,7 +127,9 @@
     chunk = 256 if point_count % 256 == 0 else 128
     rate = max(1, units // 2)
     modes_step, cubic_step = 2, 4
-    half, per, lag_end, lag_mid = slab_schedule(planes, count, units, rate, cubic_step)
+    half, inner, shared, outer = slab_owners(planes, count)
+    lag_end, lag_mid = slab_schedule(planes, count, units, rate, cubic_step)
+    tail = max(0, planes - 4)
     up = {"my": me + 1}
     down = {"my": me - 1}
     has_up = me < count - 1
@@ -145,16 +154,20 @@
     def rows(j):
         return pl.ds(pl.multiple_of(j * block, block), block)
 
+    def group_of(p):
+        return jnp.minimum(lax.div(p, 2 * inner), half - 1)
+
     def owner_of(p):
-        group = lax.div(p, 2 * per)
-        return jnp.where(lax.rem(p, 2) == 1, half + group, half - 1 - group)
+        return jnp.where(lax.rem(p, 2) == 1, half + group_of(p), half - 1 - group_of(p))
 
     def slot_of(p):
-        return lax.div(lax.rem(p, 2 * per), 2)
+        return lax.div(p - group_of(p) * (2 * inner), 2)
+
+    own_group = jnp.where(me >= half, me - half, half - 1 - me)
+    owned = jnp.where(own_group < half - 1, inner, outer)
 
     def plane_of(k):
-        group = jnp.where(me >= half, me - half, half - 1 - me)
-        return group * (2 * per) + 2 * k + (me >= half).astype(jnp.int32)
+        return own_group * (2 * inner) + 2 * k + (me >= half).astype(jnp.int32)
 
     def mode_copy(p, h, j, target_row, target):
         return pltpu.make_async_remote_copy(
@@ -228,44 +241,51 @@
 
     strips = block // 16
 
-    def coef_copy(i):
-        slot = lax.rem(i, 2)
-        strip = pl.ds(pl.multiple_of(lax.rem(i, strips) * 16, 16), 16)
-        return pltpu.make_async_copy(
-            coef_ref.at[lax.div(i, strips), :, strip], coef.at[slot], coef_sem.at[slot]
-        )
+    def coef_copy(i, part):
+        strip = pl.ds(pl.multiple_of(i * 16, 16), 16)
+        return pltpu.make_async_copy(coef_ref.at[part, :, strip], coef.at[part], coef_sem.at[part])
 
     noise_copy(0).start()
     if planes > 1:
         noise_copy(1).start()
-    coef_copy(0).start()
-    coef_copy(1).start()
+    coef_copy(0, 0).start()
+    coef_copy(0, 1).start()
 
     pl.semaphore_wait(barrier, len(line_peers) + len(rep_peers))
 
+    def split_table():
+        split[...] = jnp.zeros_like(split)
+        for h in range(row_count):
+            for part in range(2):
+                for t in range(full + (1 if rest else 0)):
+                    size = min(128, row_block - t * 128)
+                    source = h * row_block + t * 128
+                    place = (h * (full + (1 if rest else 0)) + t) * 128 + (part * rest if size < 128 else 0)
+                    split[part, place : place + size] = table_ref[source : source + size]
+
     def contract_strip(i, carry):
-        coef_copy(i).wait()
-        part = lax.div(i, strips)
-        strip = pl.ds(pl.multiple_of(lax.rem(i, strips) * 16, 16), 16)
-        wide[...] = jnp.dot(
-            coef[lax.rem(i, 2)].reshape(row_block * 16, coef.shape[3]), slab_ref[...],
-            preferred_element_type=jnp.float32,
-        )
-
-        @pl.when(i + 2 < 2 * strips)
-        def _():
-            coef_copy(i + 2).start()
+        strip = pl.ds(pl.multiple_of(i * 16, 16), 16)
+        for part in range(2):
+            coef_copy(i, part).wait()
+            wide[part] = jnp.dot(
+                coef[part].reshape(row_block * 16, coef.shape[3]), slab_ref[...],
+                preferred_element_type=jnp.float32,
+            )
+
+            @pl.when(i + 1 < strips)
+            def _():
+                coef_copy(i + 1, part).start()
 
         for b in range(16):
-            for t, first, size in tiles:
-                turn = wide[pl.ds(first * 16 + b, size, stride=16), :].T[:planes_rep]
-                if size < 128:
-                    turn = jnp.concatenate([turn, jnp.zeros((planes_rep, 128 - size), jnp.float32)], 1)
-                spread[t, pl.ds(b, planes_rep, stride=16), :] = turn
-        for t, first, size in tiles:
-            zmodes[:, part, strip, first : first + size] = (
-                spread[t, :, :size].reshape(planes_rep, 16, size).astype(jnp.bfloat16)
-            )
+            for part in range(2):
+                for t in range(full):
+                    turn = wide[part, pl.ds(t * 2048 + b, 128, stride=16), :].T[:planes_rep]
+                    spread[part * full + t, pl.ds(b, planes_rep, stride=16), :] = turn
+            if rest:
+                both = [wide[part, pl.ds(full * 2048 + b, rest, stride=16), :] for part in range(2)]
+                spread[2 * full, pl.ds(b, planes_rep, stride=16), :] = jnp.concatenate(both, 0).T[:planes_rep]
+        for t in range(pieces):
+            zmodes[:, t, strip, :] = spread[t].reshape(planes_rep, 16, 128).astype(jnp.bfloat16)
         return carry
 
     def send_modes(p, carry):
@@ -286,6 +306,11 @@
 
     def inside(p):
         return jnp.logical_and(p >= 0, p < planes)
+
+    def span_of(i):
+        low = jnp.where(i == planes - 1, tail, i)
+        valid = jnp.logical_and(i >= 0, jnp.logical_or(i < tail, i == planes - 1))
+        return low, jnp.where(valid, i + 1, low)
 
     own_points = pl.ds(pl.multiple_of(me * point_block, point_block), point_block)
 
@@ -334,13 +359,14 @@
 
         span = pl.ds(pl.multiple_of(at * width, width), width)
         for part in range(2):
-            line = None
+            field = []
             for h in range(row_count):
-                more = jnp.dot(
-                    modes[k, h, part], table_ref[h * row_block : (h + 1) * row_block, span],
-                    preferred_element_type=jnp.float32,
-                )
-                line = more if line is None else line + more
+                field += [modes[k, h, part * full + t] for t in range(full)]
+                if rest:
+                    field.append(modes[k, h, 2 * full])
+            line = jnp.dot(
+                jnp.concatenate(field, 1), split[part, :, span], preferred_element_type=jnp.float32
+            )
             lines[:, part * width : (part + 1) * width] = line.astype(jnp.bfloat16)
         columns = None
         for first in range(0, point_count, chunk):
@@ -394,86 +420,117 @@
         def _():
             project_noise(s)
 
-        merging = s - merge_lag
+        sent = jnp.where(s < shared, s, s - lag_end)
+        at_end = jnp.logical_or(me == 0, me == count - 1)
+        merging = jnp.where(at_end, sent, s - merge_lag)
 
         @pl.when(jnp.logical_and(inside(merging), owner_of(merging) == me))
         def _():
             both = parts[merging].astype(jnp.float32) + cubic[slot_of(merging)].astype(jnp.float32)
             parts[merging] = both.astype(jnp.bfloat16)
 
-        rising = s - rise_lag
-        sinking = s - sink_lag
-
-        @pl.when(jnp.logical_and(inside(rising), me == 0))
+        low, high = span_of(sent)
+        high = jnp.where(jnp.logical_or(s < shared, sent >= shared), high, low)
+
+        @pl.when(me == 0)
         def _():
             for j in range(count - 1, 0, -1):
-                sum_copy(rising, j, 0, j).start()
-
-        @pl.when(jnp.logical_and(inside(sinking), me == count - 1))
+                def emit(p, carry):
+                    sum_copy(p, j, 0, j).start()
+                    return carry
+
+                lax.fori_loop(low, high, emit, 0)
+
+        @pl.when(me == count - 1)
         def _():
             for j in range(count - 1):
-                sum_copy(sinking, j, 1, count if j == count - 2 else j).start()
+                def emit(p, carry):
+                    sum_copy(p, j, 1, count if j == count - 2 else j).start()
+                    return carry
+
+                lax.fori_loop(low, high, emit, 0)
 
         @pl.when(s == modes_step)
         def _():
-            lax.fori_loop(0, 2 * strips, contract_strip, 0)
+            lax.fori_loop(0, strips, contract_strip, 0)
             lax.fori_loop(0, planes, send_modes, 0)
 
         unit = (s - cubic_step) * rate
         lax.fori_loop(
-            jnp.clip(unit, 0, per * units), jnp.clip(unit + rate, 0, per * units), cubic_unit, 0
-        )
-
+            jnp.clip(unit, 0, owned * units), jnp.clip(unit + rate, 0, owned * units), cubic_unit, 0
+        )
+
+        low, high = span_of(s - rise_lag)
         for far in range(count - 2, 0, -1):
-            @pl.when(jnp.logical_and(jnp.logical_and(inside(rising), has_down), me + far <= count - 1))
+            @pl.when(jnp.logical_and(has_down, me + far <= count - 1))
             def _():
                 j = me + far
-                sum_copy(rising, j, 0, j).wait_recv()
-                add(rising, j, j)
-                sum_copy(rising, j, 0, j).start()
-
+
+                def relay(p, carry):
+                    sum_copy(p, j, 0, j).wait_recv()
+                    add(p, j, j)
+                    sum_copy(p, j, 0, j).start()
+                    return carry
+
+                lax.fori_loop(low, high, relay, 0)
+
+        low, high = span_of(s - sink_lag)
         for far in range(count - 2, 0, -1):
-            @pl.when(jnp.logical_and(jnp.logical_and(inside(sinking), has_up), me - far >= 0))
+            @pl.when(jnp.logical_and(has_up, me - far >= 0))
             def _():
                 j = me - far
-                sum_copy(sinking, j, 1, j).wait_recv()
-                add(sinking, j, j)
-                sum_copy(sinking, j, 1, count if far == 1 else j).start()
-
-        done = s - done_lag
-
-        @pl.when(inside(done))
-        def _():
+
+                def relay(p, carry):
+                    sum_copy(p, j, 1, j).wait_recv()
+                    add(p, j, j)
+                    sum_copy(p, j, 1, count if far == 1 else j).start()
+                    return carry
+
+                lax.fori_loop(low, high, relay, 0)
+
+        def finish_plane(p, carry):
             @pl.when(has_down)
             def _():
-                sum_copy(done, me, 0, me).wait_recv()
-                add(done, me, me)
+                sum_copy(p, me, 0, me).wait_recv()
+                add(p, me, me)
 
             @pl.when(has_up)
             def _():
-                sum_copy(done, me, 1, count).wait_recv()
-                add(done, me, count)
-
-            for part in range(2):
-                whole = parts[done, part, rows(me)]
-                for h in range(row_count):
-                    halves[done, h, part] = whole[:, h * row_block : (h + 1) * row_block]
+                sum_copy(p, me, 1, count).wait_recv()
+                add(p, me, count)
+
+            whole = [parts[p, part, rows(me)] for part in range(2)]
+            for h in range(row_count):
+                for part in range(2):
+                    for t in range(full):
+                        place = h * row_block + t * 128
+                        halves[p, h, part * full + t] = whole[part][:, place : place + 128]
+                if rest:
+                    place = h * row_block + full * 128
+                    halves[p, h, 2 * full] = jnp.concatenate(
+                        [whole[part][:, place : place + rest] for part in range(2)], 1
+                    )
             for at in range(len(spots) - 1, -1, -1):
-                first_copy(done, at, False).start()
+                first_copy(p, at, False).start()
             if pair == 2:
-                second_copy(done, 0, False).start()
-
-        passing = done - 1
-
-        @pl.when(inside(passing))
-        def _():
+                second_copy(p, 0, False).start()
+            return carry
+
+        low, high = span_of(s - done_lag)
+        lax.fori_loop(low, high, finish_plane, 0)
+
+        def pass_on(p, carry):
             for at in range(1, len(spots)):
-                first_copy(passing, at, True).wait_recv()
+                first_copy(p, at, True).wait_recv()
                 if pair == 2:
-                    second_copy(passing, at, False).start()
-
+                    second_copy(p, at, False).start()
+            return carry
+
+        low, high = span_of(s - done_lag - 1)
+        lax.fori_loop(low, high, pass_on, 0)
         return carry
 
+    split_table()
     lax.fori_loop(0, planes + lag_mid + count - 1, step, 0)
 
     def finish(p, carry):
@@ -516,7 +573,9 @@
     _, row_block, block, depth = coefficients.shape
     planes = noise_field.shape[0]
     planes_rep = planes * row_count
-    per = planes // count
+    outer = slab_owners(planes, count)[3]
+    pieces = 2 * row_block // 128
+    places = row_count * pl.cdiv(row_block, 128) * 128
     spots = row_count * (rep_count // (2 if rep_count % 2 == 0 else 1))
     point_block, point_count = noise_field.shape[2:]
     width = max(c for c in (256, 128) if point_count % c == 0)
@@ -527,25 +586,26 @@
     flops = 12 * planes * mode_count * point_block * (point_count + mode_count)
     return pl.pallas_call(
         slab_kernel,
-        out_shape=jax.ShapeDtypeStruct((planes_rep * rep_count, 2, block, row_block), jnp.bfloat16),
+        out_shape=jax.ShapeDtypeStruct((planes_rep * rep_count, pieces, block, 128), jnp.bfloat16),
         in_specs=[hbm, hbm, vmem, vmem, vmem],
         out_specs=hbm,
         scratch_shapes=[
             pltpu.VMEM((2, row_block, 16, depth), jnp.bfloat16),
-            pltpu.VMEM((row_block * 16, lanes), jnp.float32),
-            pltpu.VMEM((pl.cdiv(row_block, 128), planes_rep * 16, 128), jnp.float32),
-            pltpu.VMEM((planes_rep, 2, block, row_block), jnp.bfloat16),
-            pltpu.VMEM((per, row_count, 2, mode_count, row_block), jnp.bfloat16),
+            pltpu.VMEM((2, row_block * 16, lanes), jnp.float32),
+            pltpu.VMEM((pieces, planes_rep * 16, 128), jnp.float32),
+            pltpu.VMEM((planes_rep, pieces, block, 128), jnp.bfloat16),
+            pltpu.VMEM((outer, row_count, pieces, mode_count, 128), jnp.bfloat16),
+            pltpu.VMEM((2, places, point_count), jnp.bfloat16),
             pltpu.VMEM((mode_count, 2 * width), jnp.bfloat16),
             pltpu.VMEM((2, mode_count, mode_count), jnp.float32),
-            pltpu.VMEM((per, 2, mode_count, mode_count), jnp.bfloat16),
+            pltpu.VMEM((outer, 2, mode_count, mode_count), jnp.bfloat16),
             pltpu.VMEM((planes, 2, mode_count, mode_count), jnp.bfloat16),
             pltpu.VMEM((planes, count + 1, 2, block, mode_count), jnp.bfloat16),
             pltpu.VMEM((2, 2, point_block, point_count), jnp.bfloat16),
-            pltpu.VMEM((planes, row_count, 2, block, row_block), jnp.bfloat16),
+            pltpu.VMEM((planes, row_count, pieces, block, 128), jnp.bfloat16),
             dma((2,)),
             dma((2,)),
-            dma((per, row_count, count)),
+            dma((outer, row_count, count)),
             dma((planes, row_count)),
             dma((planes, count + 1)),
             dma((planes, 2, count)),
@@ -580,7 +640,8 @@
     own_block = mode_count // rep_count
     if (
         col_block % 16 or row_block % 16 or point_block % 128 or mode_count % 128
-        or col_count < 2 or col_count % 2 or planes_dev % col_count or planes_rep > 128 or planes_rep % 8
+        or row_block % 64 or col_count < 2 or col_count % 2 or planes_dev % (2 * col_count)
+        or planes_rep > 128 or planes_rep % 8
     ):
         return plain_body(coefficients, noise_field, mode_table)
     slab_own = lax.dynamic_slice_in_dim(
@@ -591,8 +652,16 @@
     slab_back = lax.dynamic_slice_in_dim(mode_table, rep_index * own_block, own_block, 0)[
         :, slab_first : slab_first + planes_all
     ]
-    summed = jnp.einsum("zpba,nz->pabn", plane_grid, slab_back, preferred_element_type=jnp.float32)
-    return summed.astype(jnp.bfloat16)
+    summed = jnp.einsum("ztbl,nz->tlbn", plane_grid, slab_back, preferred_element_type=jnp.float32)
+    summed = summed.astype(jnp.bfloat16)
+    full, rest = row_block // 128, row_block % 128
+    halves = []
+    for part in range(2):
+        lines = [summed[part * full + t] for t in range(full)]
+        if rest:
+            lines.append(summed[2 * full, part * rest : (part + 1) * rest])
+        halves.append(jnp.concatenate(lines, 0))
+    return jnp.stack(halves)
 
 
 def solution(mesh):

time: 274 us -> 296 us (1.080)
  other arithmetic: 0 us -> 14.4 us
  Pallas kernels: 239 us -> 253 us
  matrix products: 16.8 us -> 7.95 us
    another operation x0 -> x2, other arithmetic: none -> 14.4 us  [body(): return jnp.stack(halves)]
    pallas_call x1, Pallas kernels: 239 us -> 253 us  [slab_planes(): pl.pallas_call(slab_kernel, out_shape=jax.ShapeDtypeStruct((planes_rep *...]
    another operation x0 -> x1, local copies, waits for them, and re-layouts: none -> 13.9 us  [body(): return jnp.stack(halves)]
    convert_element_type x1 -> x0, local copies, waits for them, and re-layouts: 13.9 us -> none  [body(): return summed.astype(jnp.bfloat16)]
    dot_general x1, matrix products: 16.8 us -> 7.95 us  [body(): jnp.einsum('ztbl,nz->tlbn', plane_grid, slab_back, preferred_element_type...]
where the time goes in v3:
time: 296 us; the launch traced here: 295 us
  Pallas kernels  253 us (85%)
  local copies, waits for them, and re-layouts  19.5 us (7%)
  other arithmetic  14.4 us (5%)
  matrix products  7.95 us (3%)
    pallas_call x1, Pallas kernels, slab_planes(): pl.pallas_call(slab_kernel, out_shape=jax.ShapeDtypeStruct((planes_rep *...  253 us
    another operation x2, other arithmetic, body(): return jnp.stack(halves)  14.4 us
    another operation x1, local copies, waits for them, and re-layouts, body(): return jnp.stack(halves)  13.9 us
    dot_general x1, matrix products, body(): jnp.einsum('ztbl,nz->tlbn', plane_grid, slab_back, preferred_element_type...  7.95 us

profile of v3, /device:TPU:0, one launch (start us, length us, event | category | flops | bytes accessed | tf_op | source)
XLA Modules:
  0.0 295.4 jit_solution(17787789952879609247)
XLA Ops:
  0.0 1.0 constant_dynamic-slice_fusion
  1.0 0.7 pad.4.slab_ref
  1.7 2.4 copy.4
  4.0 253.5 %shard_map.37 = bf16[128,3,96,128]{3,2,1,0:T(8,128)(2,1)} custom-call(bf16[2,192,96,384]{3,2,1,0:T(8,128)(2,1)} %coef_ref.1, bf16[16,2,384,1536]{3,2,1,0:T(8,128)(2,1)} %noise_ref.1, bf16[384,1536]{1,0:T(8,128)(2,1)} %table_ref.1, bf16[1536,384]{1,0:T(8,128)(2,1)} %bitcast.20, bf16[384,128]{1,0:T(8,128)(2,1)} %pad.4.slab_ref), custom_call_target="tpu_custom_call" | custom-call | flops 54358179840 | bytes 37748736 | tf_op jit(solution)/shard_map/pallas_call | solution.py:587
  257.5 7.9 %convert_bitcast_fusion = bf16[3,128,96,96]{1,3,2,0:T(8,128)(2,1)S(1)} fusion(bf16[128,3,96,128]{3,2,1,0:T(8,128)(2,1)} %shard_map.37, bf16[384,1536]{1,0:T(8,128)(2,1)} %table_ref.1, s32[]{:T(128)S(6)} %select_n.6, s32[]{:T(128)S(6)} %add.12), kind=kOutput, calls=%fused_computation.3 | convolution fusion | flops 909508608 | bytes 16539656 | tf_op jit(solution)/shard_map/ztbl,nz->tlbn/dot_general | solution.py:655
  265.5 0.8 slice_bitcast_fusion.2
  266.3 0.8 slice_bitcast_fusion.3
  267.1 5.2 %maximum_bitcast_fusion = (bf16[1,192,96,96]{1,3,2,0:T(8,128)(2,1)}, bf16[1,192,96,96]{1,3,2,0:T(8,128)(2,1)}) fusion(bf16[64,96,96]{0,2,1:T(8,128)(2,1)S(1)} %get-tuple-element.7, bf16[128,96,96]{0,2,1:T(8,128)(2,1)S(1)} %get-tuple-element.5, bf16[64,96,96]{0,2,1:T(8,128)(2,1)S(1)} %get-tuple-element.8, bf16[128,96,96]{0,2,1:T(8,128)(2,1)S(1)} %get-tuple-element.6), kind=kLoop, calls=%fused_computation.4 | loop fusion | flops 14155776 | bytes 14155776 | tf_op jit(solution)/shard_map/stack | solution.py:664
  272.3 9.2 %pad_maximum_fusion = bf16[2,192,96,96]{1,3,2,0:T(8,128)(2,1)} fusion(bf16[1,192,96,96]{1,3,2,0:T(8,128)(2,1)} %get-tuple-element.10, bf16[1,192,96,96]{1,3,2,0:T(8,128)(2,1)} %get-tuple-element.9), kind=kLoop, calls=%fused_computation | loop fusion | flops 3538944 | bytes 14155776 | tf_op jit(solution)/shard_map/stack | solution.py:664
  281.5 13.9 %copy.6 = bf16[2,192,96,96]{3,2,1,0:T(8,128)(2,1)} copy(bf16[2,192,96,96]{1,3,2,0:T(8,128)(2,1)} %pad_maximum_fusion) | data formatting | bytes 14155776 | tf_op jit(solution)/shard_map/stack | solution.py:664

commit v4 on v3

--- a/solution.py
+++ b/solution.py
@@ -78,7 +78,7 @@
 
 def slab_owners(planes, count):
     half = count // 2
-    inner = max(1, planes // count // 2)
+    inner = max(1, 3 * planes // (4 * count))
     shared = 2 * inner * (half - 1)
     return half, inner, shared, (planes - shared) // 2
 
@@ -124,12 +124,12 @@
     point_block = noise_ref.shape[2]
     width = lines.shape[1] // 2
     units = point_count // width
-    chunk = 256 if point_count % 256 == 0 else 128
+    chunk = max(c for c in (512, 256, 128) if point_count % c == 0)
     rate = max(1, units // 2)
-    modes_step, cubic_step = 2, 4
+    modes_step, cubic_step = 2, 6
     half, inner, shared, outer = slab_owners(planes, count)
     lag_end, lag_mid = slab_schedule(planes, count, units, rate, cubic_step)
-    tail = max(0, planes - 4)
+    tail = max(0, planes - 2)
     up = {"my": me + 1}
     down = {"my": me - 1}
     has_up = me < count - 1
@@ -288,7 +288,12 @@
             zmodes[:, t, strip, :] = spread[t].reshape(planes_rep, 16, 128).astype(jnp.bfloat16)
         return carry
 
-    def send_modes(p, carry):
+    def send_modes(i, carry):
+        turn = lax.div(i, 2)
+        even = min(shared, planes - shared) // 2
+        later = turn - even + (0 if shared > planes - shared else shared // 2)
+        mixed = lax.div(turn, 2) + lax.rem(turn, 2) * (shared // 2)
+        p = 2 * jnp.where(turn < 2 * even, mixed, later) + lax.rem(i, 2)
         target = owner_of(p)
         for dh in range(row_count):
             target_row = lax.rem(row + dh, row_count)
@@ -623,6 +628,64 @@
     )(coefficients, noise_field, mode_table, turned, slab_own)
 
 
+def update_kernel(grid_ref, slab_ref, out_ref, wide, lines):
+    planes, pieces, strip, lanes = grid_ref.shape
+    _, row_block, _, own_block = out_ref.shape
+    full = row_block // lanes
+    rest = row_block % lanes
+    for t in range(pieces):
+        wide[t] = grid_ref[:, t].astype(jnp.float32).reshape(planes * strip, lanes)
+    for t in range(pieces):
+        for b in range(0, strip, 2):
+            pair = [
+                wide[t, pl.ds(b + e, planes, stride=strip), :].astype(jnp.bfloat16) for e in range(2)
+            ]
+            both = jnp.dot(
+                slab_ref[...], jnp.concatenate(pair, 1), preferred_element_type=jnp.float32
+            )
+            for e in range(2):
+                turn = both[:, e * lanes : (e + 1) * lanes].T
+                if t < 2 * full:
+                    first = (t % full) * lanes * strip + b + e
+                    lines[t // full, pl.ds(first, lanes, stride=strip), :] = turn
+                else:
+                    first = full * lanes * strip + b + e
+                    for part in range(2):
+                        lines[part, pl.ds(first, rest, stride=strip), :] = turn[
+                            part * rest : (part + 1) * rest
+                        ]
+    for part in range(2):
+        out_ref[part] = (
+            lines[part, :, :own_block].reshape(row_block, strip, own_block).astype(jnp.bfloat16)
+        )
+
+
+def update_planes(plane_grid, slab_back, row_block):
+    planes, pieces, block, lanes = plane_grid.shape
+    own_block = slab_back.shape[0]
+    strip = 16
+    slab = jnp.pad(slab_back, ((0, lanes - own_block), (0, 0)))
+    return pl.pallas_call(
+        update_kernel,
+        grid=(block // strip,),
+        out_shape=jax.ShapeDtypeStruct((2, row_block, block, own_block), jnp.bfloat16),
+        in_specs=[
+            pl.BlockSpec((planes, pieces, strip, lanes), lambda b: (0, 0, b, 0)),
+            pl.BlockSpec((lanes, planes), lambda b: (0, 0)),
+        ],
+        out_specs=pl.BlockSpec((2, row_block, strip, own_block), lambda b: (0, 0, b, 0)),
+        scratch_shapes=[
+            pltpu.VMEM((pieces, planes * strip, lanes), jnp.float32),
+            pltpu.VMEM((2, row_block * strip, lanes), jnp.float32),
+        ],
+        compiler_params=pltpu.CompilerParams(vmem_limit_bytes=60 * 1024 * 1024),
+        cost_estimate=pl.CostEstimate(
+            flops=4 * planes * row_block * block * own_block, bytes_accessed=plane_grid.size * 2,
+            transcendentals=0,
+        ),
+    )(plane_grid, slab)
+
+
 def body(coefficients, noise_field, mode_table):
     rep_index = lax.axis_index("rep")
     rep_count = lax.axis_size("rep")
@@ -641,7 +704,7 @@
     if (
         col_block % 16 or row_block % 16 or point_block % 128 or mode_count % 128
         or row_block % 64 or col_count < 2 or col_count % 2 or planes_dev % (2 * col_count)
-        or planes_rep > 128 or planes_rep % 8
+        or planes_rep > 128 or planes_rep % 8 or planes_all % 8 or own_block > 128
     ):
         return plain_body(coefficients, noise_field, mode_table)
     slab_own = lax.dynamic_slice_in_dim(
@@ -652,16 +715,7 @@
     slab_back = lax.dynamic_slice_in_dim(mode_table, rep_index * own_block, own_block, 0)[
         :, slab_first : slab_first + planes_all
     ]
-    summed = jnp.einsum("ztbl,nz->tlbn", plane_grid, slab_back, preferred_element_type=jnp.float32)
-    summed = summed.astype(jnp.bfloat16)
-    full, rest = row_block // 128, row_block % 128
-    halves = []
-    for part in range(2):
-        lines = [summed[part * full + t] for t in range(full)]
-        if rest:
-            lines.append(summed[2 * full, part * rest : (part + 1) * rest])
-        halves.append(jnp.concatenate(lines, 0))
-    return jnp.stack(halves)
+    return update_planes(plane_grid, slab_back, row_block)
 
 
 def solution(mesh):

time: 296 us -> 232 us (0.78)
  Pallas kernels: 253 us -> 226 us
  other arithmetic: 14.4 us -> 0 us
  local copies, waits for them, and re-layouts: 19.5 us -> 5.5 us
  matrix products: 7.95 us -> 0 us
    pallas_call x1, Pallas kernels: 253 us -> 210 us  [slab_planes(): pl.pallas_call(slab_kernel, out_shape=jax.ShapeDtypeStruct((planes_rep *...]
    pallas_call x0 -> x1, Pallas kernels: none -> 15.9 us  [update_planes(): pl.pallas_call(update_kernel, grid=(block // strip,), out_shape=jax.Shape...]
    another operation x2 -> x0, other arithmetic: 14.4 us -> none  [body(): return jnp.stack(halves)]
    another operation x1 -> x0, local copies, waits for them, and re-layouts: 13.9 us -> none  [body(): return jnp.stack(halves)]
    dot_general x1 -> x0, matrix products: 7.95 us -> none  [body(): jnp.einsum('ztbl,nz->tlbn', plane_grid, slab_back, preferred_element_type...]
where the time goes in v4:
time: 232 us; the launch traced here: 231 us
  Pallas kernels  226 us (97%)
  local copies, waits for them, and re-layouts  5.5 us (2%)
    pallas_call x1, Pallas kernels, slab_planes(): pl.pallas_call(slab_kernel, out_shape=jax.ShapeDtypeStruct((planes_rep *...  210 us
    pallas_call x1, Pallas kernels, update_planes(): pl.pallas_call(update_kernel, grid=(block // strip,), out_shape=jax.Shape...  15.9 us

profile of v4, /device:TPU:0, one launch (start us, length us, event | category | flops | bytes accessed | tf_op | source)
XLA Modules:
  0.0 231.4 jit_solution(461326580384739876)
XLA Ops:
  0.0 0.9 dynamic-slice
  0.9 0.6 pad.9.slab_ref
  1.5 1.0 constant_dynamic-slice_fusion
  2.5 0.7 pad.8.slab_ref
  3.1 2.4 %copy.4 = bf16[384,1536]{0,1:T(8,128)(2,1)} copy(bf16[384,1536]{1,0:T(8,128)(2,1)} %table_ref.1) | data formatting | bytes 2359296 | tf_op args[2]
  5.5 209.9 %shard_map.37.grid_ref = bf16[128,3,96,128]{3,2,1,0:T(8,128)(2,1)} custom-call(bf16[2,192,96,384]{3,2,1,0:T(8,128)(2,1)} %coef_ref.1, bf16[16,2,384,1536]{3,2,1,0:T(8,128)(2,1)} %noise_ref.1, bf16[384,1536]{1,0:T(8,128)(2,1)} %table_ref.1, bf16[1536,384]{1,0:T(8,128)(2,1)} %bitcast.1, bf16[384,128]{1,0:T(8,128)(2,1)} %pad.8.slab_ref), custom_call_target="tpu_custom_call" | custom-call | flops 54358179840 | bytes 37748736 | tf_op jit(solution)/shard_map/pallas_call | solution.py:592
  215.5 15.9 %shard_map.38 = bf16[2,192,96,96]{3,2,1,0:T(8,128)(2,1)} custom-call(bf16[128,3,96,128]{3,2,1,0:T(8,128)(2,1)} %shard_map.37.grid_ref, bf16[128,128]{1,0:T(8,128)(2,1)} %pad.9.slab_ref), custom_call_target="tpu_custom_call" | custom-call | flops 905969664 | bytes 9437184 | tf_op jit(solution)/shard_map/pallas_call | solution.py:668

commit v5 on v4

--- a/solution.py
+++ b/solution.py
@@ -78,7 +78,7 @@
 
 def slab_owners(planes, count):
     half = count // 2
-    inner = max(1, 3 * planes // (4 * count))
+    inner = max(1, planes // (2 * count))
     shared = 2 * inner * (half - 1)
     return half, inner, shared, (planes - shared) // 2
 
@@ -98,8 +98,8 @@
     return lag_end, lag_mid
 
 
-def slab_kernel(coef_ref, noise_ref, table_ref, turned_ref, slab_ref, out_ref, coef, wide, spread, zmodes,
-                modes, split, lines, total, cubic, parts, landed, noise, halves, coef_sem, noise_sem, mode_recv,
+def slab_kernel(coef_ref, noise_ref, table_ref, out_ref, back_ref, coef, wide, spread, zmodes, modes, split,
+                turned_ref, slab_ref, lines, total, cubic, parts, landed, noise, halves, coef_sem, noise_sem, mode_recv,
                 mode_send, sum_recv, sum_send, first_recv, first_send, second_recv, second_send):
     count = lax.axis_size("my")
     me = lax.axis_index("my")
@@ -126,7 +126,7 @@
     units = point_count // width
     chunk = max(c for c in (512, 256, 128) if point_count % c == 0)
     rate = max(1, units // 2)
-    modes_step, cubic_step = 2, 6
+    modes_step, cubic_step = 2, 5
     half, inner, shared, outer = slab_owners(planes, count)
     lag_end, lag_mid = slab_schedule(planes, count, units, rate, cubic_step)
     tail = max(0, planes - 2)
@@ -251,9 +251,27 @@
     coef_copy(0, 0).start()
     coef_copy(0, 1).start()
 
-    pl.semaphore_wait(barrier, len(line_peers) + len(rep_peers))
-
-    def split_table():
+    def selected(source, offset, wanted):
+        shape = (source.shape[1], 128)
+        source_at = lax.broadcasted_iota(jnp.int32, shape, 0)
+        target_at = lax.broadcasted_iota(jnp.int32, shape, 1)
+        chosen = jnp.logical_and(source_at == target_at + offset, target_at < wanted)
+        return jnp.dot(
+            source, chosen.astype(jnp.float32).astype(jnp.bfloat16), preferred_element_type=jnp.float32
+        ).astype(jnp.bfloat16)
+
+    def prepare_tables():
+        planes_all = planes_rep * rep_count
+        slab_first = point_count // 2 - planes_all // 2
+        base = slab_first // 128 * 128
+        window = slice(base, pl.cdiv(slab_first + planes_all, 128) * 128)
+        slab_ref[...] = selected(table_ref[:, window], slab_first - base + rep * planes_rep, planes_rep)
+        own_block = mode_count // rep_count
+        own_rows = pl.ds(pl.multiple_of(rep * own_block, own_block), own_block)
+        back = selected(table_ref[own_rows, window], slab_first - base, planes_all)
+        back_ref[...] = jnp.concatenate([back, jnp.zeros((128 - own_block, 128), jnp.bfloat16)], 0)
+        for first in range(0, point_count, 128):
+            turned_ref[first : first + 128] = table_ref[:, first : first + 128].T
         split[...] = jnp.zeros_like(split)
         for h in range(row_count):
             for part in range(2):
@@ -329,12 +347,12 @@
             field = noise[slot, :, :, span].reshape(2 * point_block, step_of)
             more = lax.dot_general(table_ref[:, span], field, NT, preferred_element_type=jnp.float32)
             columns = more if columns is None else columns + more
-        turned = turned_ref[own_points]
+        own_table = table_ref[:, own_points]
         for part in range(2):
             column = columns[:, part * point_block : (part + 1) * point_block].astype(jnp.bfloat16)
-            parts[p, part] = jnp.dot(column, turned, preferred_element_type=jnp.float32).astype(
-                jnp.bfloat16
-            )
+            parts[p, part] = lax.dot_general(
+                column, own_table, NT, preferred_element_type=jnp.float32
+            ).astype(jnp.bfloat16)
 
         @pl.when(p + 2 < planes)
         def _():
@@ -421,10 +439,6 @@
     done_lag = jnp.maximum(rise_lag, sink_lag)
 
     def step(s, carry):
-        @pl.when(s < planes)
-        def _():
-            project_noise(s)
-
         sent = jnp.where(s < shared, s, s - lag_end)
         at_end = jnp.logical_or(me == 0, me == count - 1)
         merging = jnp.where(at_end, sent, s - merge_lag)
@@ -457,8 +471,13 @@
 
         @pl.when(s == modes_step)
         def _():
+            prepare_tables()
             lax.fori_loop(0, strips, contract_strip, 0)
             lax.fori_loop(0, planes, send_modes, 0)
+
+        @pl.when(s + 1 < planes)
+        def _():
+            project_noise(s + 1)
 
         unit = (s - cubic_step) * rate
         lax.fori_loop(
@@ -535,7 +554,8 @@
         lax.fori_loop(low, high, pass_on, 0)
         return carry
 
-    split_table()
+    project_noise(0)
+    pl.semaphore_wait(barrier, len(line_peers) + len(rep_peers))
     lax.fori_loop(0, planes + lag_mid + count - 1, step, 0)
 
     def finish(p, carry):
@@ -570,7 +590,7 @@
     lax.fori_loop(0, planes, finish, 0)
 
 
-def slab_planes(coefficients, noise_field, mode_table, turned, slab_own):
+def slab_planes(coefficients, noise_field, mode_table):
     count = lax.axis_size("my")
     mode_count = mode_table.shape[0]
     row_count = lax.axis_size("mx")
@@ -584,23 +604,27 @@
     spots = row_count * (rep_count // (2 if rep_count % 2 == 0 else 1))
     point_block, point_count = noise_field.shape[2:]
     width = max(c for c in (256, 128) if point_count % c == 0)
-    lanes = slab_own.shape[1]
     vmem = pl.BlockSpec(memory_space=pltpu.VMEM)
     hbm = pl.BlockSpec(memory_space=pl.ANY)
     dma = pltpu.SemaphoreType.DMA
     flops = 12 * planes * mode_count * point_block * (point_count + mode_count)
     return pl.pallas_call(
         slab_kernel,
-        out_shape=jax.ShapeDtypeStruct((planes_rep * rep_count, pieces, block, 128), jnp.bfloat16),
-        in_specs=[hbm, hbm, vmem, vmem, vmem],
-        out_specs=hbm,
+        out_shape=(
+            jax.ShapeDtypeStruct((planes_rep * rep_count, pieces, block, 128), jnp.bfloat16),
+            jax.ShapeDtypeStruct((128, 128), jnp.bfloat16),
+        ),
+        in_specs=[hbm, hbm, vmem],
+        out_specs=(hbm, vmem),
         scratch_shapes=[
             pltpu.VMEM((2, row_block, 16, depth), jnp.bfloat16),
-            pltpu.VMEM((2, row_block * 16, lanes), jnp.float32),
+            pltpu.VMEM((2, row_block * 16, 128), jnp.float32),
             pltpu.VMEM((pieces, planes_rep * 16, 128), jnp.float32),
             pltpu.VMEM((planes_rep, pieces, block, 128), jnp.bfloat16),
             pltpu.VMEM((outer, row_count, pieces, mode_count, 128), jnp.bfloat16),
             pltpu.VMEM((2, places, point_count), jnp.bfloat16),
+            pltpu.VMEM((point_count, mode_count), jnp.bfloat16),
+            pltpu.VMEM((depth, 128), jnp.bfloat16),
             pltpu.VMEM((mode_count, 2 * width), jnp.bfloat16),
             pltpu.VMEM((2, mode_count, mode_count), jnp.float32),
             pltpu.VMEM((outer, 2, mode_count, mode_count), jnp.bfloat16),
@@ -625,7 +649,7 @@
         cost_estimate=pl.CostEstimate(
             flops=flops, bytes_accessed=noise_field.size * 2, transcendentals=0
         ),
-    )(coefficients, noise_field, mode_table, turned, slab_own)
+    )(coefficients, noise_field, mode_table)
 
 
 def update_kernel(grid_ref, slab_ref, out_ref, wide, lines):
@@ -660,11 +684,9 @@
         )
 
 
-def update_planes(plane_grid, slab_back, row_block):
+def update_planes(plane_grid, slab_back, row_block, own_block):
     planes, pieces, block, lanes = plane_grid.shape
-    own_block = slab_back.shape[0]
     strip = 16
-    slab = jnp.pad(slab_back, ((0, lanes - own_block), (0, 0)))
     return pl.pallas_call(
         update_kernel,
         grid=(block // strip,),
@@ -683,11 +705,10 @@
             flops=4 * planes * row_block * block * own_block, bytes_accessed=plane_grid.size * 2,
             transcendentals=0,
         ),
-    )(plane_grid, slab)
+    )(plane_grid, slab_back)
 
 
 def body(coefficients, noise_field, mode_table):
-    rep_index = lax.axis_index("rep")
     rep_count = lax.axis_size("rep")
     row_count = lax.axis_size("mx")
     col_count = lax.axis_size("my")
@@ -696,7 +717,6 @@
     planes_all = planes_rep * rep_count
     mode_count = mode_table.shape[0]
     point_count = mode_table.shape[1]
-    slab_first = point_count // 2 - planes_all // 2
     row_block = mode_count // row_count
     col_block = mode_count // col_count
     point_block = point_count // col_count
@@ -704,18 +724,11 @@
     if (
         col_block % 16 or row_block % 16 or point_block % 128 or mode_count % 128
         or row_block % 64 or col_count < 2 or col_count % 2 or planes_dev % (2 * col_count)
-        or planes_rep > 128 or planes_rep % 8 or planes_all % 8 or own_block > 128
+        or planes_rep % 8 or planes_all != 128 or own_block > 128 or own_block % 16
     ):
         return plain_body(coefficients, noise_field, mode_table)
-    slab_own = lax.dynamic_slice_in_dim(
-        mode_table, slab_first + rep_index * planes_rep, planes_rep, 1
-    )
-    slab_own = jnp.pad(slab_own, ((0, 0), (0, 128 - planes_rep)))
-    plane_grid = slab_planes(coefficients, noise_field, mode_table, mode_table.T, slab_own)
-    slab_back = lax.dynamic_slice_in_dim(mode_table, rep_index * own_block, own_block, 0)[
-        :, slab_first : slab_first + planes_all
-    ]
-    return update_planes(plane_grid, slab_back, row_block)
+    plane_grid, slab_back = slab_planes(coefficients, noise_field, mode_table)
+    return update_planes(plane_grid, slab_back, row_block, own_block)
 
 
 def solution(mesh):

time: 232 us -> 222 us (0.957)
  local copies, waits for them, and re-layouts: 5.5 us -> 0 us
  Pallas kernels: 226 us -> 222 us
    pallas_call x1, Pallas kernels: 210 us -> 206 us  [slab_planes(): pl.pallas_call(slab_kernel, out_shape=(jax.ShapeDtypeStruct((planes_rep *...]
    unnamed x1 -> x0, local copies, waits for them, and re-layouts: 2.37 us -> none
where the time goes in v5:
time: 222 us
  Pallas kernels  222 us (100%)
    pallas_call x1, Pallas kernels, slab_planes(): pl.pallas_call(slab_kernel, out_shape=(jax.ShapeDtypeStruct((planes_rep *...  206 us
    pallas_call x1, Pallas kernels, update_planes(): pl.pallas_call(update_kernel, grid=(block // strip,), out_shape=jax.Shape...  15.9 us

profile of v5, /device:TPU:0, one launch (start us, length us, event | category | flops | bytes accessed | tf_op | source)
XLA Modules:
  0.0 222.0 jit_solution(12277812892409421223)
XLA Ops:
  0.0 206.0 %shard_map.37 = (bf16[128,3,96,128]{3,2,1,0:T(8,128)(2,1)}, bf16[128,128]{1,0:T(8,128)(2,1)}) custom-call(bf16[2,192,96,384]{3,2,1,0:T(8,128)(2,1)} %coef_ref.1, bf16[16,2,384,1536]{3,2,1,0:T(8,128)(2,1)} %noise_ref.1, bf16[384,1536]{1,0:T(8,128)(2,1)} %table_ref.1), custom_call_target="tpu_custom_call" | custom-call | flops 54358179840 | bytes 37748736 | tf_op jit(solution)/shard_map/pallas_call | solution.py:611
  206.0 15.9 %shard_map.38 = bf16[2,192,96,96]{3,2,1,0:T(8,128)(2,1)} custom-call(bf16[128,3,96,128]{3,2,1,0:T(8,128)(2,1)} %get-tuple-element.7.grid_ref, bf16[128,128]{1,0:T(8,128)(2,1)} %get-tuple-element.8.slab_ref), custom_call_target="tpu_custom_call" | custom-call | flops 905969664 | bytes 9437184 | tf_op jit(solution)/shard_map/pallas_call | solution.py:690

commit v6 on v5

--- a/solution.py
+++ b/solution.py
@@ -260,12 +260,12 @@
             source, chosen.astype(jnp.float32).astype(jnp.bfloat16), preferred_element_type=jnp.float32
         ).astype(jnp.bfloat16)
 
+    planes_all = planes_rep * rep_count
+    slab_first = point_count // 2 - planes_all // 2
+    base = slab_first // 128 * 128
+    window = slice(base, pl.cdiv(slab_first + planes_all, 128) * 128)
+
     def prepare_tables():
-        planes_all = planes_rep * rep_count
-        slab_first = point_count // 2 - planes_all // 2
-        base = slab_first // 128 * 128
-        window = slice(base, pl.cdiv(slab_first + planes_all, 128) * 128)
-        slab_ref[...] = selected(table_ref[:, window], slab_first - base + rep * planes_rep, planes_rep)
         own_block = mode_count // rep_count
         own_rows = pl.ds(pl.multiple_of(rep * own_block, own_block), own_block)
         back = selected(table_ref[own_rows, window], slab_first - base, planes_all)
@@ -310,7 +310,7 @@
         turn = lax.div(i, 2)
         even = min(shared, planes - shared) // 2
         later = turn - even + (0 if shared > planes - shared else shared // 2)
-        mixed = lax.div(turn, 2) + lax.rem(turn, 2) * (shared // 2)
+        mixed = lax.div(turn, 2) + (1 - lax.rem(turn, 2)) * (shared // 2)
         p = 2 * jnp.where(turn < 2 * even, mixed, later) + lax.rem(i, 2)
         target = owner_of(p)
         for dh in range(row_count):
@@ -471,9 +471,12 @@
 
         @pl.when(s == modes_step)
         def _():
-            prepare_tables()
+            slab_ref[...] = selected(
+                table_ref[:, window], slab_first - base + rep * planes_rep, planes_rep
+            )
             lax.fori_loop(0, strips, contract_strip, 0)
             lax.fori_loop(0, planes, send_modes, 0)
+            prepare_tables()
 
         @pl.when(s + 1 < planes)
         def _():

time: 222 us -> 221 us (level)
  no operation moved by 1% of the time
where the time goes in v6:
time: 221 us
  Pallas kernels  221 us (100%)
    pallas_call x1, Pallas kernels, slab_planes(): pl.pallas_call(slab_kernel, out_shape=(jax.ShapeDtypeStruct((planes_rep *...  205 us
    pallas_call x1, Pallas kernels, update_planes(): pl.pallas_call(update_kernel, grid=(block // strip,), out_shape=jax.Shape...  15.9 us

profile of v6, /device:TPU:0, one launch (start us, length us, event | category | flops | bytes accessed | tf_op | source)
XLA Modules:
  0.0 220.9 jit_solution(7479402681277804645)
XLA Ops:
  0.0 205.0 %shard_map.37 = (bf16[128,3,96,128]{3,2,1,0:T(8,128)(2,1)}, bf16[128,128]{1,0:T(8,128)(2,1)}) custom-call(bf16[2,192,96,384]{3,2,1,0:T(8,128)(2,1)} %coef_ref.1, bf16[16,2,384,1536]{3,2,1,0:T(8,128)(2,1)} %noise_ref.1, bf16[384,1536]{1,0:T(8,128)(2,1)} %table_ref.1), custom_call_target="tpu_custom_call" | custom-call | flops 54358179840 | bytes 37748736 | tf_op jit(solution)/shard_map/pallas_call | solution.py:614
  205.0 15.9 %shard_map.38 = bf16[2,192,96,96]{3,2,1,0:T(8,128)(2,1)} custom-call(bf16[128,3,96,128]{3,2,1,0:T(8,128)(2,1)} %get-tuple-element.7.grid_ref, bf16[128,128]{1,0:T(8,128)(2,1)} %get-tuple-element.8.slab_ref), custom_call_target="tpu_custom_call" | custom-call | flops 905969664 | bytes 9437184 | tf_op jit(solution)/shard_map/pallas_call | solution.py:693
